TPU v7x, 256 devices: a whole 4x4x8 slice. The times are simulated.
256 devices in a mesh: sec: 4 (over z_hi), row: 8 (over x, core), col: 8 (over y, z_lo).
Axes of the slice: x: 4, y: 4, z: 8 (z_hi: 4, z_lo: 2; z = z_hi * 2 + z_lo), core: 2. Of those that a mesh axis runs over, the one named last changes fastest.
Arguments:
- vel_modes: float32 [3, 2, 4, 1024, 1024], P(None, None, 'sec', 'row', 'col'), may hold values from -0.005859375 to 0.005859375
- scalar: float32 [4, 2048, 2048], P('sec', 'row', 'col'), may hold values from -6 to 6
- obstacle: int32 [4, 16, 16], P('sec', 'row', 'col'), may hold values from 0 to 2
Outputs:
- scalar_next: float32 [4, 2048, 2048], P('sec', 'row', 'col')
All inputs are finite; a program needn't handle non-finite values.
Results may differ from a plain program's by a relative error of at most 0.00005.
Values sent between devices are 32-bit elements; how exact they have to be, the bound alone decides.
A program may use at most 64 MiB of HBM per device.

v0:
```python
import math

import jax
import jax.numpy as jnp
import numpy as np
from jax import lax
from jax.experimental import pallas as pl
from jax.experimental.pallas import tpu as pltpu
from jax.sharding import PartitionSpec as P

NV = 1024
NS = 2048
ROWS = 8
COLS = 8
SECS = 4
F32 = jnp.float32
BF16 = jnp.bfloat16
MESH = pl.DeviceIdType.MESH
HALF_ROOT = math.sqrt(0.5)


def split_pair(table):
    high = table.astype(BF16)
    low = (table - high.astype(np.float64)).astype(BF16)
    return high, low


def tables():
    k = np.arange(NV)
    k = np.where(k < NV // 2, k, k - NV)
    s = np.arange(256)
    turn = 2.0 * math.pi / NS * ((k[:, None] * s[None, :]) % NS)
    x_high, x_low = split_pair(np.concatenate([np.cos(turn), np.sin(turn)], 1))
    m = np.arange(128)
    m = np.where(m < 64, m, m - 128)
    turn = 2.0 * math.pi / 256 * ((s[:, None] * m[None, :]) % 256)
    c, d = np.cos(turn), np.sin(turn)
    y_high, y_low = split_pair(np.block([[c, -d], [d, c]]))
    lanes = np.arange(128)
    turn = 2.0 * math.pi / 8 * ((np.arange(8)[:, None] * lanes[None, :]) % 8)
    phases = np.concatenate([np.cos(turn), np.sin(turn)], 0).astype(np.float32)
    q = np.arange(8)
    turn = 2.0 * math.pi / NS * (s[:, None] * q[None, :])
    twiddles = np.concatenate([np.cos(turn), np.sin(turn)], 1).astype(np.float32)
    return x_high, x_low, y_high, y_low, phases, twiddles


def split(value):
    high = value.astype(BF16)
    return high, (value - high.astype(F32)).astype(BF16)


def kernel(modes, scalar, obstacle, x_high_in, x_low_in, y_high, y_low, phases, twiddles, out,
           arrived, x_high, x_low, lhs, sent, spectra, rhs, waves, twist, fields, velocity,
           padded, edges_out, edges_in, planes, base, slopes,
           table_sem, mode_sem, spectra_sem, velocity_sem, halo_sem, plane_sem, send_sem):
    sec, row, col = lax.axis_index("sec"), lax.axis_index("row"), lax.axis_index("col")
    place = row * COLS + col
    own_part = lax.rem(row, 4)
    own_half = lax.div(row, 4)

    loads = (pltpu.make_async_copy(scalar.at[0], padded.at[pl.ds(8, 256)], table_sem.at[0]),
             pltpu.make_async_copy(x_high_in, x_high, table_sem.at[1]),
             pltpu.make_async_copy(x_low_in, x_low, table_sem.at[2]))
    for load in loads:
        load.start()

    def own_modes(p):
        return pltpu.make_async_copy(
            modes.at[p, :, 0, pl.ds(pl.multiple_of(16 * col, 16), 16), :], arrived.at[p, col], mode_sem.at[p])

    for p in range(3):
        own_modes(p).start()

    barrier = pltpu.get_barrier_semaphore()

    def greet(i, carry):
        peer = lax.rem(place + i, ROWS * COLS)
        pl.semaphore_signal(barrier, inc=1, device_id=(sec, lax.div(peer, COLS), lax.rem(peer, COLS)), device_id_type=MESH)
        return carry

    lax.fori_loop(1, ROWS * COLS, greet, 0)
    for step in (1, 3):
        pl.semaphore_signal(barrier, inc=1, device_id=(lax.rem(sec + step, SECS), row, col), device_id_type=MESH)
    pl.semaphore_wait(barrier, ROWS * COLS + 1)

    def send_modes(i, carry):
        p = lax.div(i, COLS - 1)
        peer = lax.rem(col + 1 + lax.rem(i, COLS - 1), COLS)
        pltpu.make_async_remote_copy(
            modes.at[p, :, 0, pl.ds(pl.multiple_of(16 * peer, 16), 16), :], arrived.at[p, col],
            send_sem.at[0], mode_sem.at[p], device_id=(sec, row, peer), device_id_type=MESH).start()
        return carry

    lax.fori_loop(0, 3 * (COLS - 1), send_modes, 0)

    row_next, row_last = lax.rem(row + 1, ROWS), lax.rem(row + ROWS - 1, ROWS)
    col_next, col_last = lax.rem(col + 1, COLS), lax.rem(col + COLS - 1, COLS)
    loads[0].wait()
    edges_out[0] = padded[pl.ds(8, 256), pl.ds(128, 128)].T[120:128]
    edges_out[1] = padded[pl.ds(8, 256), pl.ds(0, 128)].T[0:8]
    halo_copies = (
        pltpu.make_async_remote_copy(scalar.at[0, pl.ds(248, 8)], padded.at[pl.ds(0, 8)], send_sem.at[3], halo_sem.at[0],
                                     device_id=(sec, row_next, col), device_id_type=MESH),
        pltpu.make_async_remote_copy(scalar.at[0, pl.ds(0, 8)], padded.at[pl.ds(264, 8)], send_sem.at[4], halo_sem.at[1],
                                     device_id=(sec, row_last, col), device_id_type=MESH),
        pltpu.make_async_remote_copy(edges_out.at[0], edges_in.at[0], send_sem.at[5], halo_sem.at[2],
                                     device_id=(sec, row, col_next), device_id_type=MESH),
        pltpu.make_async_remote_copy(edges_out.at[1], edges_in.at[1], send_sem.at[6], halo_sem.at[3],
                                     device_id=(sec, row, col_last), device_id_type=MESH),
    )
    for copy in halo_copies:
        copy.start()

    for q in range(1, 8):
        twist[0, q - 1] = jnp.broadcast_to(twiddles[:, q:q + 1], (256, 128))
        twist[1, q - 1] = jnp.broadcast_to(twiddles[:, 8 + q:9 + q], (256, 128))

    loads[1].wait()
    loads[2].wait()

    def transform_x(p, carry):
        pltpu.make_async_copy(arrived.at[p], arrived.at[p], mode_sem.at[p]).wait()
        for a in range(8):
            real, imag = arrived[p, a, 0], arrived[p, a, 1]
            for block in range(8):
                cosine, sine = phases[block:block + 1, :], phases[8 + block:9 + block, :]
                if block == 0:
                    turned = (real, imag)
                else:
                    turned = (real * cosine - imag * sine, real * sine + imag * cosine)
                for part in range(2):
                    high, low = split(turned[part])
                    lhs[pl.ds((block * 2 + part) * 16, 16), pl.ds(128 * a, 128)] = high
                    lhs[pl.ds(256 + (block * 2 + part) * 16, 16), pl.ds(128 * a, 128)] = low
        main = jnp.dot(lhs[...], x_high[...], preferred_element_type=F32)
        rest = jnp.dot(lhs[pl.ds(0, 256), :], x_low[...], preferred_element_type=F32)
        total = main[:256] + main[256:] + rest
        for block in range(8):
            real, imag = total[32 * block:32 * block + 16], total[32 * block + 16:32 * block + 32]
            new_real = real[:, :256] - imag[:, 256:]
            new_imag = real[:, 256:] + imag[:, :256]
            for half in range(2):
                sent[p, block, half, 0] = new_real[:, 128 * half:128 * half + 128]
                sent[p, block, half, 1] = new_imag[:, 128 * half:128 * half + 128]

        def send_spectra(i, inner):
            block = lax.rem(col + lax.div(i, 2), COLS)
            half = lax.rem(i, 2)
            owner = 4 * half + p
            rows = pl.ds(pl.multiple_of(16 * place, 16), 16)

            @pl.when((block != col) | (owner != row))
            def _():
                pltpu.make_async_remote_copy(
                    sent.at[p, block, half], spectra.at[:, rows, :], send_sem.at[1], spectra_sem,
                    device_id=(sec, owner, block), device_id_type=MESH).start()

            @pl.when((block == col) & (owner == row))
            def _():
                spectra[:, rows, :] = sent[p, block, half]

            return inner

        lax.fori_loop(0, 16, send_spectra, 0)
        return carry

    lax.fori_loop(0, 3, transform_x, 0)

    up = pltpu.make_async_remote_copy(scalar.at[0], planes.at[0], send_sem.at[7], plane_sem.at[0],
                                      device_id=(lax.rem(sec + 1, SECS), row, col), device_id_type=MESH)
    down = pltpu.make_async_remote_copy(scalar.at[0], planes.at[1], send_sem.at[8], plane_sem.at[1],
                                        device_id=(lax.rem(sec + SECS - 1, SECS), row, col), device_id_type=MESH)

    @pl.when(sec < SECS - 1)
    def _():
        up.start()

    @pl.when(sec > 0)
    def _():
        down.start()

    @pl.when(sec == 0)
    def _():
        planes[0] = jnp.zeros((256, 256), F32)

    @pl.when(sec == SECS - 1)
    def _():
        planes[1] = jnp.zeros((256, 256), F32)

    for copy in halo_copies:
        copy.wait()
    left_edge = edges_in[0].T[:, 7:8]
    right_edge = edges_in[1].T[:, 0:1]
    lane = lax.broadcasted_iota(jnp.int32, (128, 256), 1)
    for block in range(2):
        at = 8 + 128 * block
        here = padded[pl.ds(at, 128), :]
        left = jnp.where(lane == 0, left_edge[128 * block:128 * block + 128], pltpu.roll(here, 1, 1))
        right = jnp.where(lane == 255, right_edge[128 * block:128 * block + 128], pltpu.roll(here, 255, 1))
        back = padded[pl.ds(at - 1, 128), :]
        front = padded[pl.ds(at + 1, 128), :]
        flag = jnp.where(lane < 128, obstacle[0, block, 0].astype(F32), obstacle[0, block, 1].astype(F32))
        rows = pl.ds(128 * block, 128)
        slopes[0, rows, :] = right - left
        slopes[1, rows, :] = front - back
        base[rows, :] = here + 0.04 * (left + right + back + front - 6.0 * here) - 0.25 * flag * (here - 1.0)

    @pl.when(own_part < 3)
    def _():
        pltpu.make_async_copy(spectra.at[:, pl.ds(0, 1008), :], spectra.at[:, pl.ds(0, 1008), :], spectra_sem).wait()
        for q in range(8):
            for part in range(2):
                high, low = split(spectra[part, pl.ds(q, 128, stride=8), :])
                rhs[pl.ds(128 * part, 128), pl.ds(128 * q, 128)] = high
                rhs[pl.ds(256 + 128 * part, 128), pl.ds(128 * q, 128)] = low
        waves[...] = (jnp.dot(y_high[...], rhs[pl.ds(0, 256), :], preferred_element_type=F32)
                      + jnp.dot(y_high[...], rhs[pl.ds(256, 256), :], preferred_element_type=F32)
                      + jnp.dot(y_low[...], rhs[pl.ds(0, 256), :], preferred_element_type=F32))

        def combine(i, carry):
            at = pl.multiple_of(16 * i, 16)
            rows = pl.ds(at, 16)
            real, imag = [], []
            for q in range(8):
                re = waves[rows, pl.ds(128 * q, 128)]
                if q == 0:
                    real.append(re)
                    imag.append(None)
                    continue
                im = waves[pl.ds(256 + at, 16), pl.ds(128 * q, 128)]
                cosine, sine = twist[0, q - 1, rows, :], twist[1, q - 1, rows, :]
                real.append(re * cosine - im * sine)
                imag.append(None if q == 4 else re * sine + im * cosine)
            a1, b1 = real[1] + real[7], imag[1] - imag[7]
            a2, b2 = real[2] + real[6], imag[2] - imag[6]
            a3, b3 = real[3] + real[5], imag[3] - imag[5]
            even, odd = real[0] + real[4], real[0] - real[4]
            e0, e2, e1, e3 = even + a2, even - a2, odd - b2, odd + b2
            d0, d2 = a1 + a3, b3 - b1
            amid, bmid = HALF_ROOT * (a1 - a3), HALF_ROOT * (b1 + b3)
            d1, d3 = amid - bmid, -amid - bmid
            for r, (e, d) in enumerate(((e0, d0), (e1, d1), (e2, d2), (e3, d3))):
                fields[r, rows, :] = e + d
                fields[r + 4, rows, :] = e - d
            return carry

        lax.fori_loop(0, 16, combine, 0)

        def send_fields(i, carry):
            peer = lax.rem(row + i, ROWS)
            pltpu.make_async_remote_copy(
                fields.at[peer], velocity.at[own_part, own_half], send_sem.at[2], velocity_sem.at[own_part],
                device_id=(sec, peer, col), device_id_type=MESH).start()
            return carry

        lax.fori_loop(1, ROWS, send_fields, 0)
        velocity[own_part, own_half] = fields[row]

    @pl.when(sec > 0)
    def _():
        up.wait_recv()

    @pl.when(sec < SECS - 1)
    def _():
        down.wait_recv()

    slopes[2] = planes[1] - planes[0]
    base[...] = base[...] + 0.04 * (planes[1] + planes[0])

    for p in range(3):
        one = pltpu.make_async_copy(velocity.at[p, 0], velocity.at[p, 0], velocity_sem.at[p])
        two = pltpu.make_async_copy(velocity.at[p], velocity.at[p], velocity_sem.at[p])
        pl.when(own_part == p)(one.wait)
        pl.when(own_part != p)(two.wait)
    for half in range(2):
        lanes = pl.ds(128 * half, 128)
        out[0, :, lanes] = base[:, lanes] - 0.125 * (
            velocity[0, half] * slopes[0, :, lanes] + velocity[1, half] * slopes[1, :, lanes]
            + velocity[2, half] * slopes[2, :, lanes])

    sent_modes = arrived.at[:, pl.ds(0, 7)]
    pltpu.make_async_copy(sent_modes, sent_modes, send_sem.at[0]).wait()

    @pl.when(own_part < 3)
    def _():
        some = spectra.at[:, pl.ds(0, 47 * 16), :]
        pltpu.make_async_copy(some, some, send_sem.at[1]).wait()
        most = fields.at[pl.ds(0, 7)]
        pltpu.make_async_copy(most, most, send_sem.at[2]).wait()

    @pl.when(own_part == 3)
    def _():
        some = spectra.at[:, pl.ds(0, 48 * 16), :]
        pltpu.make_async_copy(some, some, send_sem.at[1]).wait()

    @pl.when(sec < SECS - 1)
    def _():
        up.wait_send()

    @pl.when(sec > 0)
    def _():
        down.wait_send()


def body(modes, scalar, obstacle):
    x_high, x_low, y_high, y_low, phases, twiddles = (jnp.asarray(t) for t in tables())
    anywhere = pl.BlockSpec(memory_space=pl.ANY)
    vmem = pl.BlockSpec(memory_space=pltpu.VMEM)
    smem = pl.BlockSpec(memory_space=pltpu.SMEM)
    dma = pltpu.SemaphoreType.DMA
    return pl.pallas_call(
        kernel,
        out_shape=jax.ShapeDtypeStruct((1, 256, 256), F32),
        in_specs=[anywhere, anywhere, smem, anywhere, anywhere, vmem, vmem, vmem, vmem],
        out_specs=vmem,
        scratch_shapes=[
            pltpu.VMEM((3, 8, 2, 16, 128), F32),
            pltpu.VMEM((1024, 512), BF16),
            pltpu.VMEM((1024, 512), BF16),
            pltpu.VMEM((512, 1024), BF16),
            pltpu.VMEM((3, 8, 2, 2, 16, 128), F32),
            pltpu.VMEM((2, 1024, 128), F32),
            pltpu.VMEM((512, 1024), BF16),
            pltpu.VMEM((512, 1024), F32),
            pltpu.VMEM((2, 7, 256, 128), F32),
            pltpu.VMEM((8, 256, 128), F32),
            pltpu.VMEM((3, 2, 256, 128), F32),
            pltpu.VMEM((272, 256), F32),
            pltpu.VMEM((2, 8, 256), F32),
            pltpu.VMEM((2, 8, 256), F32),
            pltpu.VMEM((2, 256, 256), F32),
            pltpu.VMEM((256, 256), F32),
            pltpu.VMEM((3, 256, 256), F32),
            dma((3,)), dma((3,)), dma, dma((3,)), dma((4,)), dma((2,)), dma((9,)),
        ],
        compiler_params=pltpu.CompilerParams(
            collective_id=0, has_side_effects=True, vmem_limit_bytes=56 * 1024 * 1024),
    )(modes, scalar, obstacle, x_high, x_low, y_high, y_low, phases, twiddles)


def solution(mesh):
    in_specs = (P(None, None, "sec", "row", "col"), P("sec", "row", "col"), P("sec", "row", "col"))
    out_specs = P("sec", "row", "col")
    return jax.shard_map(body, mesh=mesh, in_specs=in_specs, out_specs=out_specs, check_vma=False)
```

profile of v0, /device:TPU:1, one launch (start us, length us, event | category | flops | bytes accessed | tf_op | source)
XLA Modules:
  0.0 49.7 jit_solution(16779693937570166288)
XLA Ops:
  0.0 48.0 %shard_map.91 = f32[1,256,256]{2,1,0:T(8,128)} custom-call(f32[3,2,1,128,128]{4,3,2,1,0:T(8,128)} %modes.1, f32[1,256,256]{2,1,0:T(8,128)} %scalar.1, s32[1,2,2]{2,1,0:T(2,128)} %obstacle.1, bf16[1024,512]{1,0:T(8,128)(2,1)} %constant.12.clone.x_high_in, bf16[1024,512]{1,0:T(8,128)(2,1)} %constant.13.clone.x_low_in, bf16[512,256]{1,0:T(8,128)(2,1)} %constant.14.clone.y_high, ...), custom_call_target="tpu_custom_call" | custom-call | tf_op jit(solution)/shard_map/pallas_call | solution.py:312
  48.0 1.7 %copy.11 = f32[1,256,256]{2,1,0:T(8,128)} copy(f32[1,256,256]{2,1,0:T(8,128)} %shard_map.91) | data formatting | bytes 524288
where the time goes:
time: 49.8 us; the launch traced here: 49.7 us
  Pallas kernels  48 us (96%)
  local copies, waits for them, and re-layouts  1.67 us (3%)
    pallas_call x1, Pallas kernels, body(): pl.pallas_call(kernel, out_shape=jax.ShapeDtypeStruct((1, 256, 256), F32)...  48 us
    unnamed x1, local copies, waits for them, and re-layouts  1.67 us

commit v1 on v0

--- a/solution.py
+++ b/solution.py
@@ -50,77 +50,87 @@
     return high, (value - high.astype(F32)).astype(BF16)
 
 
-def kernel(modes, scalar, obstacle, x_high_in, x_low_in, y_high, y_low, phases, twiddles, out,
-           arrived, x_high, x_low, lhs, sent, spectra, rhs, waves, twist, fields, velocity,
+def kernel(modes_in, scalar, obstacle, x_high_in, x_low_in, y_high_in, y_low_in, phases_in, twiddles_in, out,
+           modes, arrived, x_high, x_low, y_high, y_low, phases, twiddles, lhs, sent, spectra, rhs, waves, twist, fields, velocity,
            padded, edges_out, edges_in, planes, base, slopes,
-           table_sem, mode_sem, spectra_sem, velocity_sem, halo_sem, plane_sem, send_sem):
+           table_sem, mode_sem, spectra_sem, velocity_sem, halo_sem, plane_sem, send_sem, ready_sem):
     sec, row, col = lax.axis_index("sec"), lax.axis_index("row"), lax.axis_index("col")
-    place = row * COLS + col
-    own_part = lax.rem(row, 4)
-    own_half = lax.div(row, 4)
-
-    loads = (pltpu.make_async_copy(scalar.at[0], padded.at[pl.ds(8, 256)], table_sem.at[0]),
-             pltpu.make_async_copy(x_high_in, x_high, table_sem.at[1]),
-             pltpu.make_async_copy(x_low_in, x_low, table_sem.at[2]))
+
+    barrier = pltpu.get_barrier_semaphore()
+
+    def at_row(i):
+        return (sec, lax.rem(row + i, ROWS), col)
+
+    def at_col(i):
+        return (sec, row, lax.rem(col + i, COLS))
+
+    for i in range(1, 8):
+        pl.semaphore_signal(barrier, inc=1, device_id=at_col(i), device_id_type=MESH)
+        pl.semaphore_signal(barrier, inc=1, device_id=at_row(i), device_id_type=MESH)
+    for step in (1, 3):
+        pl.semaphore_signal(barrier, inc=1, device_id=(lax.rem(sec + step, SECS), row, col), device_id_type=MESH)
+
+    pairs = ((modes_in, modes), (scalar.at[0], padded.at[pl.ds(8, 256)]), (twiddles_in, twiddles), (phases_in, phases),
+             (x_high_in, x_high), (x_low_in, x_low), (y_high_in, y_high), (y_low_in, y_low))
+    loads = [pltpu.make_async_copy(here, there, table_sem.at[i]) for i, (here, there) in enumerate(pairs)]
     for load in loads:
         load.start()
 
-    def own_modes(p):
-        return pltpu.make_async_copy(
-            modes.at[p, :, 0, pl.ds(pl.multiple_of(16 * col, 16), 16), :], arrived.at[p, col], mode_sem.at[p])
-
-    for p in range(3):
-        own_modes(p).start()
-
-    barrier = pltpu.get_barrier_semaphore()
-
-    def greet(i, carry):
-        peer = lax.rem(place + i, ROWS * COLS)
-        pl.semaphore_signal(barrier, inc=1, device_id=(sec, lax.div(peer, COLS), lax.rem(peer, COLS)), device_id_type=MESH)
-        return carry
-
-    lax.fori_loop(1, ROWS * COLS, greet, 0)
-    for step in (1, 3):
-        pl.semaphore_signal(barrier, inc=1, device_id=(lax.rem(sec + step, SECS), row, col), device_id_type=MESH)
-    pl.semaphore_wait(barrier, ROWS * COLS + 1)
-
-    def send_modes(i, carry):
-        p = lax.div(i, COLS - 1)
-        peer = lax.rem(col + 1 + lax.rem(i, COLS - 1), COLS)
-        pltpu.make_async_remote_copy(
-            modes.at[p, :, 0, pl.ds(pl.multiple_of(16 * peer, 16), 16), :], arrived.at[p, col],
-            send_sem.at[0], mode_sem.at[p], device_id=(sec, row, peer), device_id_type=MESH).start()
-        return carry
-
-    lax.fori_loop(0, 3 * (COLS - 1), send_modes, 0)
-
-    row_next, row_last = lax.rem(row + 1, ROWS), lax.rem(row + ROWS - 1, ROWS)
-    col_next, col_last = lax.rem(col + 1, COLS), lax.rem(col + COLS - 1, COLS)
+    lead = (col, col, row)
+    follow = (row, row, col)
+    lead_peer = (at_col, at_col, at_row)
+    follow_peer = (at_row, at_row, at_col)
+
     loads[0].wait()
+    for part in range(2):
+        modes[2, part, 0] = modes[2, part, 0].T
+    pl.semaphore_wait(barrier, 16)
+
+    for i in range(1, 8):
+        for p in (0, 2, 1):
+            peer = lax.rem(lead[p] + i, 8)
+            pltpu.make_async_remote_copy(
+                modes.at[p, :, 0, pl.ds(pl.multiple_of(16 * peer, 16), 16), :], arrived.at[p, lead[p]],
+                send_sem.at[0], mode_sem.at[p], device_id=lead_peer[p](i), device_id_type=MESH).start()
+    for i in range(1, 8):
+        pl.semaphore_signal(ready_sem, inc=1, device_id=at_row(i), device_id_type=MESH)
+
+    loads[1].wait()
     edges_out[0] = padded[pl.ds(8, 256), pl.ds(128, 128)].T[120:128]
     edges_out[1] = padded[pl.ds(8, 256), pl.ds(0, 128)].T[0:8]
     halo_copies = (
         pltpu.make_async_remote_copy(scalar.at[0, pl.ds(248, 8)], padded.at[pl.ds(0, 8)], send_sem.at[3], halo_sem.at[0],
-                                     device_id=(sec, row_next, col), device_id_type=MESH),
+                                     device_id=at_row(1), device_id_type=MESH),
         pltpu.make_async_remote_copy(scalar.at[0, pl.ds(0, 8)], padded.at[pl.ds(264, 8)], send_sem.at[4], halo_sem.at[1],
-                                     device_id=(sec, row_last, col), device_id_type=MESH),
+                                     device_id=at_row(7), device_id_type=MESH),
         pltpu.make_async_remote_copy(edges_out.at[0], edges_in.at[0], send_sem.at[5], halo_sem.at[2],
-                                     device_id=(sec, row, col_next), device_id_type=MESH),
+                                     device_id=at_col(1), device_id_type=MESH),
         pltpu.make_async_remote_copy(edges_out.at[1], edges_in.at[1], send_sem.at[6], halo_sem.at[3],
-                                     device_id=(sec, row, col_last), device_id_type=MESH),
+                                     device_id=at_col(7), device_id_type=MESH),
     )
     for copy in halo_copies:
         copy.start()
 
+    loads[2].wait()
     for q in range(1, 8):
         twist[0, q - 1] = jnp.broadcast_to(twiddles[:, q:q + 1], (256, 128))
         twist[1, q - 1] = jnp.broadcast_to(twiddles[:, 8 + q:9 + q], (256, 128))
-
-    loads[1].wait()
-    loads[2].wait()
-
-    def transform_x(p, carry):
-        pltpu.make_async_copy(arrived.at[p], arrived.at[p], mode_sem.at[p]).wait()
+    for p in range(3):
+        arrived[p, lead[p]] = modes[p, :, 0, pl.ds(pl.multiple_of(16 * lead[p], 16), 16), :]
+    for load in loads[3:]:
+        load.wait()
+    pl.semaphore_wait(ready_sem, 7)
+
+    parity = lax.rem(row + col, 2)
+    chunk = lax.div(row, 2)
+    plain_owner = parity == 0
+    turned_owner = lax.rem(col, 4) == 1 + lax.rem(row, 2)
+    own_half = jnp.where(plain_owner, lax.rem(chunk, 2), lax.div(col, 4))
+    own_part = jnp.where(plain_owner, lax.div(chunk, 2), jnp.where(turned_owner, 2, 3))
+
+    for p in (0, 2, 1):
+        some = arrived.at[p, pl.ds(0, 7)]
+        pltpu.make_async_copy(some, some, mode_sem.at[p]).wait()
         for a in range(8):
             real, imag = arrived[p, a, 0], arrived[p, a, 1]
             for block in range(8):
@@ -144,28 +154,30 @@
                 sent[p, block, half, 0] = new_real[:, 128 * half:128 * half + 128]
                 sent[p, block, half, 1] = new_imag[:, 128 * half:128 * half + 128]
 
-        def send_spectra(i, inner):
-            block = lax.rem(col + lax.div(i, 2), COLS)
-            half = lax.rem(i, 2)
-            owner = 4 * half + p
-            rows = pl.ds(pl.multiple_of(16 * place, 16), 16)
-
-            @pl.when((block != col) | (owner != row))
-            def _():
-                pltpu.make_async_remote_copy(
-                    sent.at[p, block, half], spectra.at[:, rows, :], send_sem.at[1], spectra_sem,
-                    device_id=(sec, owner, block), device_id_type=MESH).start()
-
-            @pl.when((block == col) & (owner == row))
-            def _():
-                spectra[:, rows, :] = sent[p, block, half]
-
-            return inner
-
-        lax.fori_loop(0, 16, send_spectra, 0)
-        return carry
-
-    lax.fori_loop(0, 3, transform_x, 0)
+        rows = pl.ds(pl.multiple_of(16 * (follow[p] * 8 + lead[p]), 16), 16)
+        for i in range(8):
+            block = lax.rem(lead[p] + i, 8)
+            for half in range(2):
+                if p < 2:
+                    owner = 2 * (2 * p + half) + lax.rem(block, 2)
+                    target = (sec, owner, block)
+                else:
+                    owner = 4 * half + 1 + lax.rem(block, 2)
+                    target = (sec, block, owner)
+
+                def away():
+                    pltpu.make_async_remote_copy(
+                        sent.at[p, block, half], spectra.at[:, rows, :], send_sem.at[1], spectra_sem,
+                        device_id=target, device_id_type=MESH).start()
+
+                if i > 0:
+                    away()
+                else:
+                    pl.when(owner != follow[p])(away)
+
+                    @pl.when(owner == follow[p])
+                    def _():
+                        spectra[:, rows, :] = sent[p, block, half]
 
     up = pltpu.make_async_remote_copy(scalar.at[0], planes.at[0], send_sem.at[7], plane_sem.at[0],
                                       device_id=(lax.rem(sec + 1, SECS), row, col), device_id_type=MESH)
@@ -247,15 +259,18 @@
 
         lax.fori_loop(0, 16, combine, 0)
 
-        def send_fields(i, carry):
-            peer = lax.rem(row + i, ROWS)
-            pltpu.make_async_remote_copy(
-                fields.at[peer], velocity.at[own_part, own_half], send_sem.at[2], velocity_sem.at[own_part],
-                device_id=(sec, peer, col), device_id_type=MESH).start()
-            return carry
-
-        lax.fori_loop(1, ROWS, send_fields, 0)
-        velocity[own_part, own_half] = fields[row]
+    def send_fields(number, peers):
+        def go():
+            for i in range(1, 8):
+                peer = lax.rem(number + i, 8)
+                pltpu.make_async_remote_copy(
+                    fields.at[peer], velocity.at[own_part, own_half], send_sem.at[2], velocity_sem.at[own_part],
+                    device_id=peers(i), device_id_type=MESH).start()
+            velocity[own_part, own_half] = fields[number]
+        return go
+
+    pl.when(own_part < 2)(send_fields(row, at_row))
+    pl.when(own_part == 2)(send_fields(col, at_col))
 
     @pl.when(sec > 0)
     def _():
@@ -274,10 +289,13 @@
         pl.when(own_part == p)(one.wait)
         pl.when(own_part != p)(two.wait)
     for half in range(2):
-        lanes = pl.ds(128 * half, 128)
-        out[0, :, lanes] = base[:, lanes] - 0.125 * (
-            velocity[0, half] * slopes[0, :, lanes] + velocity[1, half] * slopes[1, :, lanes]
-            + velocity[2, half] * slopes[2, :, lanes])
+        rows = pl.ds(128 * half, 128)
+        turned = velocity[2, half].T
+        for block in range(2):
+            lanes = pl.ds(128 * block, 128)
+            out[0, rows, lanes] = base[rows, lanes] - 0.125 * (
+                velocity[0, block, rows, :] * slopes[0, rows, lanes] + velocity[1, block, rows, :] * slopes[1, rows, lanes]
+                + turned[:, 128 * block:128 * block + 128] * slopes[2, rows, lanes])
 
     sent_modes = arrived.at[:, pl.ds(0, 7)]
     pltpu.make_async_copy(sent_modes, sent_modes, send_sem.at[0]).wait()
@@ -312,12 +330,17 @@
     return pl.pallas_call(
         kernel,
         out_shape=jax.ShapeDtypeStruct((1, 256, 256), F32),
-        in_specs=[anywhere, anywhere, smem, anywhere, anywhere, vmem, vmem, vmem, vmem],
+        in_specs=[anywhere, anywhere, smem] + [anywhere] * 6,
         out_specs=vmem,
         scratch_shapes=[
+            pltpu.VMEM((3, 2, 1, 128, 128), F32),
             pltpu.VMEM((3, 8, 2, 16, 128), F32),
             pltpu.VMEM((1024, 512), BF16),
             pltpu.VMEM((1024, 512), BF16),
+            pltpu.VMEM((512, 256), BF16),
+            pltpu.VMEM((512, 256), BF16),
+            pltpu.VMEM((16, 128), F32),
+            pltpu.VMEM((256, 16), F32),
             pltpu.VMEM((512, 1024), BF16),
             pltpu.VMEM((3, 8, 2, 2, 16, 128), F32),
             pltpu.VMEM((2, 1024, 128), F32),
@@ -332,7 +355,7 @@
             pltpu.VMEM((2, 256, 256), F32),
             pltpu.VMEM((256, 256), F32),
             pltpu.VMEM((3, 256, 256), F32),
-            dma((3,)), dma((3,)), dma, dma((3,)), dma((4,)), dma((2,)), dma((9,)),
+            dma((8,)), dma((3,)), dma, dma((3,)), dma((4,)), dma((2,)), dma((9,)), pltpu.SemaphoreType.REGULAR,
         ],
         compiler_params=pltpu.CompilerParams(
             collective_id=0, has_side_effects=True, vmem_limit_bytes=56 * 1024 * 1024),

time: 49.8 us -> 46.6 us (0.936)
  Pallas kernels: 48 us -> 44.8 us
    pallas_call x1, Pallas kernels: 48 us -> 44.8 us  [body(): pl.pallas_call(kernel, out_shape=jax.ShapeDtypeStruct((1, 256, 256), F32)...]
where the time goes in v1:
time: 46.6 us; the launch traced here: 46.4 us
  Pallas kernels  44.8 us (96%)
  local copies, waits for them, and re-layouts  1.67 us (4%)
    pallas_call x1, Pallas kernels, body(): pl.pallas_call(kernel, out_shape=jax.ShapeDtypeStruct((1, 256, 256), F32)...  44.8 us
    unnamed x1, local copies, waits for them, and re-layouts  1.67 us

profile of v1, /device:TPU:1, one launch (start us, length us, event | category | flops | bytes accessed | tf_op | source)
XLA Modules:
  0.0 46.4 jit_solution(5310657421383231962)
XLA Ops:
  0.0 44.8 %shard_map.91 = f32[1,256,256]{2,1,0:T(8,128)} custom-call(f32[3,2,1,128,128]{4,3,2,1,0:T(8,128)} %modes_in.1, f32[1,256,256]{2,1,0:T(8,128)} %scalar.1, s32[1,2,2]{2,1,0:T(2,128)} %obstacle.1, bf16[1024,512]{1,0:T(8,128)(2,1)} %constant.12.clone.x_high_in, bf16[1024,512]{1,0:T(8,128)(2,1)} %constant.13.clone.x_low_in, ...), custom_call_target="tpu_custom_call" | custom-call | tf_op jit(solution)/shard_map/pallas_call | solution.py:330
  44.8 1.7 %copy.11 = f32[1,256,256]{2,1,0:T(8,128)} copy(f32[1,256,256]{2,1,0:T(8,128)} %shard_map.91) | data formatting | bytes 524288

commit v2 on v1

--- a/solution.py
+++ b/solution.py
@@ -13,6 +13,7 @@
 ROWS = 8
 COLS = 8
 SECS = 4
+EARLY = 64
 F32 = jnp.float32
 BF16 = jnp.bfloat16
 MESH = pl.DeviceIdType.MESH
@@ -53,7 +54,7 @@
 def kernel(modes_in, scalar, obstacle, x_high_in, x_low_in, y_high_in, y_low_in, phases_in, twiddles_in, out,
            modes, arrived, x_high, x_low, y_high, y_low, phases, twiddles, lhs, sent, spectra, rhs, waves, twist, fields, velocity,
            padded, edges_out, edges_in, planes, base, slopes,
-           table_sem, mode_sem, spectra_sem, velocity_sem, halo_sem, plane_sem, send_sem, ready_sem):
+           table_sem, mode_sem, spectra_sem, velocity_sem, halo_sem, plane_sem, send_sem, ready_sem, go_sem):
     sec, row, col = lax.axis_index("sec"), lax.axis_index("row"), lax.axis_index("col")
 
     barrier = pltpu.get_barrier_semaphore()
@@ -86,8 +87,8 @@
         modes[2, part, 0] = modes[2, part, 0].T
     pl.semaphore_wait(barrier, 16)
 
-    for i in range(1, 8):
-        for p in (0, 2, 1):
+    for p in (0, 2, 1):
+        for i in range(1, 8):
             peer = lax.rem(lead[p] + i, 8)
             pltpu.make_async_remote_copy(
                 modes.at[p, :, 0, pl.ds(pl.multiple_of(16 * peer, 16), 16), :], arrived.at[p, lead[p]],
@@ -128,9 +129,32 @@
     own_half = jnp.where(plain_owner, lax.rem(chunk, 2), lax.div(col, 4))
     own_part = jnp.where(plain_owner, lax.div(chunk, 2), jnp.where(turned_owner, 2, 3))
 
+    def plane_copies(piece):
+        rows = pl.ds(0, EARLY) if piece == 0 else pl.ds(EARLY, 256 - EARLY)
+        return [pltpu.make_async_remote_copy(
+            scalar.at[0, rows], planes.at[i, rows], send_sem.at[7 + 2 * piece + i], plane_sem.at[2 * piece + i],
+            device_id=(lax.rem(sec + step, SECS), row, col), device_id_type=MESH) for i, step in enumerate((1, 3))]
+
+    has_above, has_below = sec < SECS - 1, sec > 0
+
+    def send_planes(piece):
+        up, down = plane_copies(piece)
+        pl.when(has_above)(up.start)
+        pl.when(has_below)(down.start)
+
+    @pl.when(sec == 0)
+    def _():
+        planes[0] = jnp.zeros((256, 256), F32)
+
+    @pl.when(sec == SECS - 1)
+    def _():
+        planes[1] = jnp.zeros((256, 256), F32)
+
     for p in (0, 2, 1):
         some = arrived.at[p, pl.ds(0, 7)]
         pltpu.make_async_copy(some, some, mode_sem.at[p]).wait()
+        if p == 0:
+            send_planes(0)
         for a in range(8):
             real, imag = arrived[p, a, 0], arrived[p, a, 1]
             for block in range(8):
@@ -179,27 +203,6 @@
                     def _():
                         spectra[:, rows, :] = sent[p, block, half]
 
-    up = pltpu.make_async_remote_copy(scalar.at[0], planes.at[0], send_sem.at[7], plane_sem.at[0],
-                                      device_id=(lax.rem(sec + 1, SECS), row, col), device_id_type=MESH)
-    down = pltpu.make_async_remote_copy(scalar.at[0], planes.at[1], send_sem.at[8], plane_sem.at[1],
-                                        device_id=(lax.rem(sec + SECS - 1, SECS), row, col), device_id_type=MESH)
-
-    @pl.when(sec < SECS - 1)
-    def _():
-        up.start()
-
-    @pl.when(sec > 0)
-    def _():
-        down.start()
-
-    @pl.when(sec == 0)
-    def _():
-        planes[0] = jnp.zeros((256, 256), F32)
-
-    @pl.when(sec == SECS - 1)
-    def _():
-        planes[1] = jnp.zeros((256, 256), F32)
-
     for copy in halo_copies:
         copy.wait()
     left_edge = edges_in[0].T[:, 7:8]
@@ -221,6 +224,12 @@
     @pl.when(own_part < 3)
     def _():
         pltpu.make_async_copy(spectra.at[:, pl.ds(0, 1008), :], spectra.at[:, pl.ds(0, 1008), :], spectra_sem).wait()
+        send_planes(1)
+
+        @pl.when(plain_owner)
+        def _():
+            pl.semaphore_signal(go_sem, inc=1, device_id=(sec, row + 1 - 2 * lax.rem(row, 2), col), device_id_type=MESH)
+
         for q in range(8):
             for part in range(2):
                 high, low = split(spectra[part, pl.ds(q, 128, stride=8), :])
@@ -259,6 +268,14 @@
 
         lax.fori_loop(0, 16, combine, 0)
 
+    @pl.when(parity == 1)
+    def _():
+        pl.semaphore_wait(go_sem, 1)
+
+    @pl.when(own_part == 3)
+    def _():
+        send_planes(1)
+
     def send_fields(number, peers):
         def go():
             for i in range(1, 8):
@@ -272,14 +289,10 @@
     pl.when(own_part < 2)(send_fields(row, at_row))
     pl.when(own_part == 2)(send_fields(col, at_col))
 
-    @pl.when(sec > 0)
-    def _():
-        up.wait_recv()
-
-    @pl.when(sec < SECS - 1)
-    def _():
-        down.wait_recv()
-
+    for piece in range(2):
+        up, down = plane_copies(piece)
+        pl.when(has_below)(up.wait_recv)
+        pl.when(has_above)(down.wait_recv)
     slopes[2] = planes[1] - planes[0]
     base[...] = base[...] + 0.04 * (planes[1] + planes[0])
 
@@ -312,13 +325,10 @@
         some = spectra.at[:, pl.ds(0, 48 * 16), :]
         pltpu.make_async_copy(some, some, send_sem.at[1]).wait()
 
-    @pl.when(sec < SECS - 1)
-    def _():
-        up.wait_send()
-
-    @pl.when(sec > 0)
-    def _():
-        down.wait_send()
+    for piece in range(2):
+        up, down = plane_copies(piece)
+        pl.when(has_above)(up.wait_send)
+        pl.when(has_below)(down.wait_send)
 
 
 def body(modes, scalar, obstacle):
@@ -355,7 +365,7 @@
             pltpu.VMEM((2, 256, 256), F32),
             pltpu.VMEM((256, 256), F32),
             pltpu.VMEM((3, 256, 256), F32),
-            dma((8,)), dma((3,)), dma, dma((3,)), dma((4,)), dma((2,)), dma((9,)), pltpu.SemaphoreType.REGULAR,
+            dma((8,)), dma((3,)), dma, dma((3,)), dma((4,)), dma((4,)), dma((11,)), pltpu.SemaphoreType.REGULAR, pltpu.SemaphoreType.REGULAR,
         ],
         compiler_params=pltpu.CompilerParams(
             collective_id=0, has_side_effects=True, vmem_limit_bytes=56 * 1024 * 1024),

time: 46.6 us -> 45.8 us (0.983)
  the two profiles are of different devices: /device:TPU:1 before, /device:TPU:68 now
where the time goes in v2:
time: 45.8 us; the launch traced here: 45.7 us
  Pallas kernels  44 us (96%)
  local copies, waits for them, and re-layouts  1.67 us (4%)
    pallas_call x1, Pallas kernels, body(): pl.pallas_call(kernel, out_shape=jax.ShapeDtypeStruct((1, 256, 256), F32)...  44 us
    unnamed x1, local copies, waits for them, and re-layouts  1.67 us

profile of v2, /device:TPU:68, one launch (start us, length us, event | category | flops | bytes accessed | tf_op | source)
XLA Modules:
  0.0 45.7 jit_solution(583019157809470445)
XLA Ops:
  0.0 44.0 %shard_map.91 = f32[1,256,256]{2,1,0:T(8,128)} custom-call(f32[3,2,1,128,128]{4,3,2,1,0:T(8,128)} %modes_in.1, f32[1,256,256]{2,1,0:T(8,128)} %scalar.1, s32[1,2,2]{2,1,0:T(2,128)} %obstacle.1, bf16[1024,512]{1,0:T(8,128)(2,1)} %constant.12.clone.x_high_in, bf16[1024,512]{1,0:T(8,128)(2,1)} %constant.13.clone.x_low_in, ...), custom_call_target="tpu_custom_call" | custom-call | tf_op jit(solution)/shard_map/pallas_call | solution.py:340
  44.0 1.7 %copy.11 = f32[1,256,256]{2,1,0:T(8,128)} copy(f32[1,256,256]{2,1,0:T(8,128)} %shard_map.91) | data formatting | bytes 524288

commit v3 on v2

--- a/solution.py
+++ b/solution.py
@@ -31,12 +31,12 @@
     k = np.where(k < NV // 2, k, k - NV)
     s = np.arange(256)
     turn = 2.0 * math.pi / NS * ((k[:, None] * s[None, :]) % NS)
-    x_high, x_low = split_pair(np.concatenate([np.cos(turn), np.sin(turn)], 1))
-    m = np.arange(128)
-    m = np.where(m < 64, m, m - 128)
+    x_high, x_low = split_pair(np.concatenate([np.cos(turn), np.sin(turn)], 0))
+    m = np.arange(64)
     turn = 2.0 * math.pi / 256 * ((s[:, None] * m[None, :]) % 256)
     c, d = np.cos(turn), np.sin(turn)
-    y_high, y_low = split_pair(np.block([[c, -d], [d, c]]))
+    y_high, y_low = split_pair(np.block([[c, d], [d, -c]]))
+    y_high = np.concatenate([y_high, y_high], 1)
     lanes = np.arange(128)
     turn = 2.0 * math.pi / 8 * ((np.arange(8)[:, None] * lanes[None, :]) % 8)
     phases = np.concatenate([np.cos(turn), np.sin(turn)], 0).astype(np.float32)
@@ -51,10 +51,18 @@
     return high, (value - high.astype(F32)).astype(BF16)
 
 
+def flip(index, bits):
+    total = 0
+    for unit in (1, 2, 4):
+        bit = lax.rem(lax.div(index, unit), 2)
+        total = total + unit * ((1 - bit) if bits & unit else bit)
+    return total
+
+
 def kernel(modes_in, scalar, obstacle, x_high_in, x_low_in, y_high_in, y_low_in, phases_in, twiddles_in, out,
-           modes, arrived, x_high, x_low, y_high, y_low, phases, twiddles, lhs, sent, spectra, rhs, waves, twist, fields, velocity,
+           modes, row_zero, extra, arrived, x_high, x_low, y_high, y_low, phases, twiddles, lhs, lone, lone_sent, lone_row, sent, spectra, rhs, waves, twist, fields, velocity,
            padded, edges_out, edges_in, planes, base, slopes,
-           table_sem, mode_sem, spectra_sem, velocity_sem, halo_sem, plane_sem, send_sem, ready_sem, go_sem):
+           table_sem, mode_sem, extra_sem, lone_sem, spectra_sem, velocity_sem, halo_sem, plane_sem, send_sem, ready_sem, go_sem):
     sec, row, col = lax.axis_index("sec"), lax.axis_index("row"), lax.axis_index("col")
 
     barrier = pltpu.get_barrier_semaphore()
@@ -65,9 +73,10 @@
     def at_col(i):
         return (sec, row, lax.rem(col + i, COLS))
 
-    for i in range(1, 8):
-        pl.semaphore_signal(barrier, inc=1, device_id=at_col(i), device_id_type=MESH)
-        pl.semaphore_signal(barrier, inc=1, device_id=at_row(i), device_id_type=MESH)
+    greeted = [at_col(i) for i in range(1, 8)] + [(sec, 7 - row, lax.rem(col + i, COLS)) for i in range(8)]
+    greeted += [(sec, flip(row, i), c) for i in range(1, 7) for c in (col, 7 - col)]
+    for device in greeted:
+        pl.semaphore_signal(barrier, inc=1, device_id=device, device_id_type=MESH)
     for step in (1, 3):
         pl.semaphore_signal(barrier, inc=1, device_id=(lax.rem(sec + step, SECS), row, col), device_id_type=MESH)
 
@@ -79,22 +88,40 @@
 
     lead = (col, col, row)
     follow = (row, row, col)
-    lead_peer = (at_col, at_col, at_row)
-    follow_peer = (at_row, at_row, at_col)
+    upper = [lax.div(f, 4) for f in follow]
+    group = [f + u * (7 - 2 * f) for f, u in zip(follow, upper)]
+
+    def device_at(p, f, l):
+        return (sec, f, l) if p < 2 else (sec, l, f)
 
     loads[0].wait()
     for part in range(2):
         modes[2, part, 0] = modes[2, part, 0].T
-    pl.semaphore_wait(barrier, 16)
+    ahead = lax.broadcasted_iota(jnp.int32, (128, 128), 0) + lax.broadcasted_iota(jnp.int32, (128, 128), 1)
+    mirror = jnp.where(ahead == 128, 1.0, 0.0).astype(F32)
+
+    def turn_round(p):
+        def go():
+            for part in range(2):
+                block = modes[p, part, 0]
+                row_zero[p, part:part + 1] = block[0:1]
+                modes[p, part, 0] = jnp.dot(mirror, block, precision=lax.Precision.HIGHEST, preferred_element_type=F32)
+        return go
 
     for p in (0, 2, 1):
-        for i in range(1, 8):
-            peer = lax.rem(lead[p] + i, 8)
-            pltpu.make_async_remote_copy(
-                modes.at[p, :, 0, pl.ds(pl.multiple_of(16 * peer, 16), 16), :], arrived.at[p, lead[p]],
-                send_sem.at[0], mode_sem.at[p], device_id=lead_peer[p](i), device_id_type=MESH).start()
-    for i in range(1, 8):
-        pl.semaphore_signal(ready_sem, inc=1, device_id=at_row(i), device_id_type=MESH)
+        pl.when(follow[p] >= 4)(turn_round(p))
+    pl.semaphore_wait(barrier, 29)
+    for i in (1, 2, 3):
+        pl.semaphore_signal(ready_sem, inc=1, device_id=(sec, flip(row, i), col), device_id_type=MESH)
+
+    for p in (0, 2, 1):
+        slot = 8 * upper[p] + lead[p]
+        for i in range(8):
+            other = lax.rem(lead[p] + i, 8)
+            for f in ((follow[p], 7 - follow[p]) if i else (7 - follow[p],)):
+                pltpu.make_async_remote_copy(
+                    modes.at[p, :, 0, pl.ds(pl.multiple_of(8 * (2 * other + lax.div(f, 4)), 8), 8), :], arrived.at[p, slot],
+                    send_sem.at[0], mode_sem.at[p], device_id=device_at(p, f, other), device_id_type=MESH).start()
 
     loads[1].wait()
     edges_out[0] = padded[pl.ds(8, 256), pl.ds(128, 128)].T[120:128]
@@ -117,10 +144,27 @@
         twist[0, q - 1] = jnp.broadcast_to(twiddles[:, q:q + 1], (256, 128))
         twist[1, q - 1] = jnp.broadcast_to(twiddles[:, 8 + q:9 + q], (256, 128))
     for p in range(3):
-        arrived[p, lead[p]] = modes[p, :, 0, pl.ds(pl.multiple_of(16 * lead[p], 16), 16), :]
+        own = 2 * lead[p] + upper[p]
+        arrived[p, 8 * upper[p] + lead[p]] = modes[p, :, 0, pl.ds(pl.multiple_of(8 * own, 8), 8), :]
     for load in loads[3:]:
         load.wait()
-    pl.semaphore_wait(ready_sem, 7)
+    pl.semaphore_wait(ready_sem, 3)
+
+    def send_zero(p):
+        return pltpu.make_async_remote_copy(
+            row_zero.at[p], extra.at[p, lead[p]], send_sem.at[11 + p], extra_sem.at[p],
+            device_id=device_at(p, lax.rem(8 - follow[p], 4), 0), device_id_type=MESH)
+
+    for p in (0, 2, 1):
+        pl.when(follow[p] >= 4)(send_zero(p).start)
+    first = (row == 0) & (col == 0)
+    sublane = lax.broadcasted_iota(jnp.int32, (8, 128), 0)
+    special = sublane < jnp.where(first, 1, 0)
+
+    def owner_of(p, block, half):
+        if p < 2:
+            return (sec, 2 * (2 * p + half) + lax.rem(block, 2), block)
+        return (sec, block, 4 * half + 1 + lax.rem(block, 2))
 
     parity = lax.rem(row + col, 2)
     chunk = lax.div(row, 2)
@@ -151,43 +195,49 @@
         planes[1] = jnp.zeros((256, 256), F32)
 
     for p in (0, 2, 1):
-        some = arrived.at[p, pl.ds(0, 7)]
+        some = arrived.at[p, pl.ds(0, 15)]
         pltpu.make_async_copy(some, some, mode_sem.at[p]).wait()
         if p == 0:
             send_planes(0)
+
+        @pl.when((lead[p] == 0) & (follow[p] < 4))
+        def _():
+            pltpu.make_async_copy(extra.at[p], extra.at[p], extra_sem.at[p]).wait()
+            for a in range(8):
+                for part in range(2):
+                    arrived[p, 8 + a, part, 0:1] = jnp.where(follow[p] > 0, extra[p, a, part:part + 1], 0.0)
+
         for a in range(8):
-            real, imag = arrived[p, a, 0], arrived[p, a, 1]
+            plus, minus = arrived[p, a], arrived[p, 8 + a]
+            sum_real, sum_imag = plus[0] + minus[0], plus[1] + minus[1]
+            gap_real = jnp.where(special, extra[p, a, 1:2], plus[0] - minus[0])
+            gap_imag = jnp.where(special, -extra[p, a, 0:1], plus[1] - minus[1])
             for block in range(8):
                 cosine, sine = phases[block:block + 1, :], phases[8 + block:9 + block, :]
                 if block == 0:
-                    turned = (real, imag)
+                    a_real, a_imag, b_real, b_imag = sum_real, sum_imag, gap_real, gap_imag
                 else:
-                    turned = (real * cosine - imag * sine, real * sine + imag * cosine)
-                for part in range(2):
-                    high, low = split(turned[part])
-                    lhs[pl.ds((block * 2 + part) * 16, 16), pl.ds(128 * a, 128)] = high
-                    lhs[pl.ds(256 + (block * 2 + part) * 16, 16), pl.ds(128 * a, 128)] = low
+                    a_real, a_imag = sum_real * cosine - sum_imag * sine, sum_real * sine + sum_imag * cosine
+                    b_real, b_imag = gap_real * cosine - gap_imag * sine, gap_real * sine + gap_imag * cosine
+                for part, tile in enumerate(((a_real, -b_imag), (-a_imag, -b_real))):
+                    high, low = split(jnp.concatenate(tile, 0))
+                    lhs[pl.ds(16 * block, 16), pl.ds(1024 * part + 128 * a, 128)] = high
+                    lhs[pl.ds(128 + 16 * block, 16), pl.ds(1024 * part + 128 * a, 128)] = low
         main = jnp.dot(lhs[...], x_high[...], preferred_element_type=F32)
-        rest = jnp.dot(lhs[pl.ds(0, 256), :], x_low[...], preferred_element_type=F32)
-        total = main[:256] + main[256:] + rest
+        rest = jnp.dot(lhs[pl.ds(0, 128), :], x_low[...], preferred_element_type=F32)
+        total = main[:128] + main[128:] + rest
         for block in range(8):
-            real, imag = total[32 * block:32 * block + 16], total[32 * block + 16:32 * block + 32]
-            new_real = real[:, :256] - imag[:, 256:]
-            new_imag = real[:, 256:] + imag[:, :256]
             for half in range(2):
-                sent[p, block, half, 0] = new_real[:, 128 * half:128 * half + 128]
-                sent[p, block, half, 1] = new_imag[:, 128 * half:128 * half + 128]
-
-        rows = pl.ds(pl.multiple_of(16 * (follow[p] * 8 + lead[p]), 16), 16)
+                tile = total[16 * block:16 * block + 16, 128 * half:128 * half + 128]
+                sent[p, block, half, 0] = tile[:8]
+                sent[p, block, half, 1] = tile[8:]
+
+        rows = pl.ds(pl.multiple_of(8 * (16 * group[p] + 2 * lead[p] + upper[p]), 8), 8)
         for i in range(8):
             block = lax.rem(lead[p] + i, 8)
             for half in range(2):
-                if p < 2:
-                    owner = 2 * (2 * p + half) + lax.rem(block, 2)
-                    target = (sec, owner, block)
-                else:
-                    owner = 4 * half + 1 + lax.rem(block, 2)
-                    target = (sec, block, owner)
+                target = owner_of(p, block, half)
+                mine = target[1 if p < 2 else 2] == follow[p]
 
                 def away():
                     pltpu.make_async_remote_copy(
@@ -197,11 +247,37 @@
                 if i > 0:
                     away()
                 else:
-                    pl.when(owner != follow[p])(away)
-
-                    @pl.when(owner == follow[p])
+                    pl.when(jnp.logical_not(mine))(away)
+
+                    @pl.when(mine)
                     def _():
                         spectra[:, rows, :] = sent[p, block, half]
+
+    @pl.when(first)
+    def _():
+        lone[...] = jnp.zeros_like(lone)
+        for p in range(3):
+            for a in range(8):
+                real, imag = extra[p, a, 0:1], extra[p, a, 1:2]
+                cosine, sine = phases[0:8, :], phases[8:16, :]
+                lone[8 * p:8 * p + 8, pl.ds(128 * a, 128)] = real * sine + imag * cosine
+                lone[8 * p:8 * p + 8, pl.ds(1024 + 128 * a, 128)] = real * cosine - imag * sine
+        high, low = split(lone[...])
+        total = (jnp.dot(high, x_high[...], preferred_element_type=F32) + jnp.dot(low, x_high[...], preferred_element_type=F32)
+                 + jnp.dot(high, x_low[...], preferred_element_type=F32))
+        for p in range(3):
+            for block in range(8):
+                for half in range(2):
+                    tile = jnp.broadcast_to(total[8 * p + block:8 * p + block + 1, 128 * half:128 * half + 128], (8, 128))
+                    if p == block == half == 0:
+                        lone_row[...] = tile
+                        continue
+                    index = (p * 8 + block) * 2 + half
+                    lone_sent[index] = tile
+                    pltpu.make_async_remote_copy(
+                        lone_sent.at[index], lone_row, send_sem.at[14], lone_sem,
+                        device_id=(sec, 2 * (2 * p + half) + block % 2, block) if p < 2 else (sec, block, 4 * half + 1 + block % 2),
+                        device_id_type=MESH).start()
 
     for copy in halo_copies:
         copy.wait()
@@ -223,7 +299,7 @@
 
     @pl.when(own_part < 3)
     def _():
-        pltpu.make_async_copy(spectra.at[:, pl.ds(0, 1008), :], spectra.at[:, pl.ds(0, 1008), :], spectra_sem).wait()
+        pltpu.make_async_copy(spectra.at[:, pl.ds(0, 504), :], spectra.at[:, pl.ds(0, 504), :], spectra_sem).wait()
         send_planes(1)
 
         @pl.when(plain_owner)
@@ -232,12 +308,19 @@
 
         for q in range(8):
             for part in range(2):
-                high, low = split(spectra[part, pl.ds(q, 128, stride=8), :])
-                rhs[pl.ds(128 * part, 128), pl.ds(128 * q, 128)] = high
-                rhs[pl.ds(256 + 128 * part, 128), pl.ds(128 * q, 128)] = low
-        waves[...] = (jnp.dot(y_high[...], rhs[pl.ds(0, 256), :], preferred_element_type=F32)
-                      + jnp.dot(y_high[...], rhs[pl.ds(256, 256), :], preferred_element_type=F32)
-                      + jnp.dot(y_low[...], rhs[pl.ds(0, 256), :], preferred_element_type=F32))
+                high, low = split(spectra[part, pl.ds(q, 64, stride=8), :])
+                rhs[pl.ds(64 * part, 64), pl.ds(128 * q, 128)] = high
+                rhs[pl.ds(128 + 64 * part, 64), pl.ds(128 * q, 128)] = low
+        waves[...] = (jnp.dot(y_high[...], rhs[...], preferred_element_type=F32)
+                      + jnp.dot(y_low[...], rhs[pl.ds(0, 128), :], preferred_element_type=F32))
+
+        @pl.when(jnp.logical_not(first))
+        def _():
+            pltpu.make_async_copy(lone_row, lone_row, lone_sem).wait()
+
+        quarter = lax.rem(lax.broadcasted_iota(jnp.int32, (16, 128), 0), 4)
+        lone_term = (jnp.where(quarter == 0, 1.0, jnp.where(quarter == 2, -1.0, 0.0)) * spectra[1, 0:1, :]
+                     + jnp.where(quarter == 1, 1.0, jnp.where(quarter == 3, -1.0, 0.0)) * lone_row[0:1, :])
 
         def combine(i, carry):
             at = pl.multiple_of(16 * i, 16)
@@ -246,7 +329,7 @@
             for q in range(8):
                 re = waves[rows, pl.ds(128 * q, 128)]
                 if q == 0:
-                    real.append(re)
+                    real.append(re + lone_term)
                     imag.append(None)
                     continue
                 im = waves[pl.ds(256 + at, 16), pl.ds(128 * q, 128)]
@@ -310,20 +393,28 @@
                 velocity[0, block, rows, :] * slopes[0, rows, lanes] + velocity[1, block, rows, :] * slopes[1, rows, lanes]
                 + turned[:, 128 * block:128 * block + 128] * slopes[2, rows, lanes])
 
-    sent_modes = arrived.at[:, pl.ds(0, 7)]
+    sent_modes = arrived.at[:, pl.ds(0, 15)]
     pltpu.make_async_copy(sent_modes, sent_modes, send_sem.at[0]).wait()
 
     @pl.when(own_part < 3)
     def _():
-        some = spectra.at[:, pl.ds(0, 47 * 16), :]
+        some = spectra.at[:, pl.ds(0, 47 * 8), :]
         pltpu.make_async_copy(some, some, send_sem.at[1]).wait()
         most = fields.at[pl.ds(0, 7)]
         pltpu.make_async_copy(most, most, send_sem.at[2]).wait()
 
     @pl.when(own_part == 3)
     def _():
-        some = spectra.at[:, pl.ds(0, 48 * 16), :]
+        some = spectra.at[:, pl.ds(0, 48 * 8), :]
         pltpu.make_async_copy(some, some, send_sem.at[1]).wait()
+
+    for p in range(3):
+        pl.when(follow[p] >= 4)(send_zero(p).wait_send)
+
+    @pl.when(first)
+    def _():
+        some = lone_sent.at[pl.ds(1, 47)]
+        pltpu.make_async_copy(some, some, send_sem.at[14]).wait()
 
     for piece in range(2):
         up, down = plane_copies(piece)
@@ -344,17 +435,22 @@
         out_specs=vmem,
         scratch_shapes=[
             pltpu.VMEM((3, 2, 1, 128, 128), F32),
-            pltpu.VMEM((3, 8, 2, 16, 128), F32),
-            pltpu.VMEM((1024, 512), BF16),
-            pltpu.VMEM((1024, 512), BF16),
+            pltpu.VMEM((3, 8, 128), F32),
+            pltpu.VMEM((3, 8, 8, 128), F32),
+            pltpu.VMEM((3, 16, 2, 8, 128), F32),
+            pltpu.VMEM((2048, 256), BF16),
+            pltpu.VMEM((2048, 256), BF16),
             pltpu.VMEM((512, 256), BF16),
-            pltpu.VMEM((512, 256), BF16),
+            pltpu.VMEM((512, 128), BF16),
             pltpu.VMEM((16, 128), F32),
             pltpu.VMEM((256, 16), F32),
-            pltpu.VMEM((512, 1024), BF16),
-            pltpu.VMEM((3, 8, 2, 2, 16, 128), F32),
-            pltpu.VMEM((2, 1024, 128), F32),
-            pltpu.VMEM((512, 1024), BF16),
+            pltpu.VMEM((256, 2048), BF16),
+            pltpu.VMEM((32, 2048), F32),
+            pltpu.VMEM((48, 8, 128), F32),
+            pltpu.VMEM((8, 128), F32),
+            pltpu.VMEM((3, 8, 2, 2, 8, 128), F32),
+            pltpu.VMEM((2, 512, 128), F32),
+            pltpu.VMEM((256, 1024), BF16),
             pltpu.VMEM((512, 1024), F32),
             pltpu.VMEM((2, 7, 256, 128), F32),
             pltpu.VMEM((8, 256, 128), F32),
@@ -365,7 +461,7 @@
             pltpu.VMEM((2, 256, 256), F32),
             pltpu.VMEM((256, 256), F32),
             pltpu.VMEM((3, 256, 256), F32),
-            dma((8,)), dma((3,)), dma, dma((3,)), dma((4,)), dma((4,)), dma((11,)), pltpu.SemaphoreType.REGULAR, pltpu.SemaphoreType.REGULAR,
+            dma((8,)), dma((3,)), dma((3,)), dma, dma, dma((3,)), dma((4,)), dma((4,)), dma((15,)), pltpu.SemaphoreType.REGULAR, pltpu.SemaphoreType.REGULAR,
         ],
         compiler_params=pltpu.CompilerParams(
             collective_id=0, has_side_effects=True, vmem_limit_bytes=56 * 1024 * 1024),

time: 45.8 us -> 42.2 us (0.921)
  the two profiles are of different devices: /device:TPU:68 before, /device:TPU:70 now
where the time goes in v3:
time: 42.2 us; the launch traced here: 42.1 us
  Pallas kernels  40.4 us (96%)
  local copies, waits for them, and re-layouts  1.67 us (4%)
    pallas_call x1, Pallas kernels, body(): pl.pallas_call(kernel, out_shape=jax.ShapeDtypeStruct((1, 256, 256), F32)...  40.4 us
    unnamed x1, local copies, waits for them, and re-layouts  1.67 us

profile of v3, /device:TPU:70, one launch (start us, length us, event | category | flops | bytes accessed | tf_op | source)
XLA Modules:
  0.0 42.1 jit_solution(10854816980289634313)
XLA Ops:
  0.0 40.4 %shard_map.91 = f32[1,256,256]{2,1,0:T(8,128)} custom-call(f32[3,2,1,128,128]{4,3,2,1,0:T(8,128)} %modes_in.1, f32[1,256,256]{2,1,0:T(8,128)} %scalar.1, s32[1,2,2]{2,1,0:T(2,128)} %obstacle.1, bf16[2048,256]{1,0:T(8,128)(2,1)} %constant.12.clone.x_high_in, bf16[2048,256]{1,0:T(8,128)(2,1)} %constant.13.clone.x_low_in, ...), custom_call_target="tpu_custom_call" | custom-call | tf_op jit(solution)/shard_map/pallas_call | solution.py:431
  40.4 1.7 %copy.11 = f32[1,256,256]{2,1,0:T(8,128)} copy(f32[1,256,256]{2,1,0:T(8,128)} %shard_map.91) | data formatting | bytes 524288

commit v4 on v3

--- a/solution.py
+++ b/solution.py
@@ -13,7 +13,8 @@
 ROWS = 8
 COLS = 8
 SECS = 4
-EARLY = 64
+PIECES = (0,64,0,192)
+ORDER = (0,1,2)
 F32 = jnp.float32
 BF16 = jnp.bfloat16
 MESH = pl.DeviceIdType.MESH
@@ -62,8 +63,14 @@
 def kernel(modes_in, scalar, obstacle, x_high_in, x_low_in, y_high_in, y_low_in, phases_in, twiddles_in, out,
            modes, row_zero, extra, arrived, x_high, x_low, y_high, y_low, phases, twiddles, lhs, lone, lone_sent, lone_row, sent, spectra, rhs, waves, twist, fields, velocity,
            padded, edges_out, edges_in, planes, base, slopes,
-           table_sem, mode_sem, extra_sem, lone_sem, spectra_sem, velocity_sem, halo_sem, plane_sem, send_sem, ready_sem, go_sem):
+           table_sem, mode_sem, extra_sem, lone_sem, spectra_sem, velocity_sem, halo_sem, plane_sem, send_sem, ready_sem):
     sec, row, col = lax.axis_index("sec"), lax.axis_index("row"), lax.axis_index("col")
+
+    pairs = ((modes_in, modes), (scalar.at[0], padded.at[pl.ds(8, 256)]), (twiddles_in, twiddles), (phases_in, phases),
+             (x_high_in, x_high), (x_low_in, x_low), (y_high_in, y_high), (y_low_in, y_low))
+    loads = [pltpu.make_async_copy(here, there, table_sem.at[i]) for i, (here, there) in enumerate(pairs)]
+    for load in loads:
+        load.start()
 
     barrier = pltpu.get_barrier_semaphore()
 
@@ -79,12 +86,6 @@
         pl.semaphore_signal(barrier, inc=1, device_id=device, device_id_type=MESH)
     for step in (1, 3):
         pl.semaphore_signal(barrier, inc=1, device_id=(lax.rem(sec + step, SECS), row, col), device_id_type=MESH)
-
-    pairs = ((modes_in, modes), (scalar.at[0], padded.at[pl.ds(8, 256)]), (twiddles_in, twiddles), (phases_in, phases),
-             (x_high_in, x_high), (x_low_in, x_low), (y_high_in, y_high), (y_low_in, y_low))
-    loads = [pltpu.make_async_copy(here, there, table_sem.at[i]) for i, (here, there) in enumerate(pairs)]
-    for load in loads:
-        load.start()
 
     lead = (col, col, row)
     follow = (row, row, col)
@@ -108,13 +109,13 @@
                 modes[p, part, 0] = jnp.dot(mirror, block, precision=lax.Precision.HIGHEST, preferred_element_type=F32)
         return go
 
-    for p in (0, 2, 1):
+    for p in ORDER:
         pl.when(follow[p] >= 4)(turn_round(p))
     pl.semaphore_wait(barrier, 29)
     for i in (1, 2, 3):
         pl.semaphore_signal(ready_sem, inc=1, device_id=(sec, flip(row, i), col), device_id_type=MESH)
 
-    for p in (0, 2, 1):
+    for p in ORDER:
         slot = 8 * upper[p] + lead[p]
         for i in range(8):
             other = lax.rem(lead[p] + i, 8)
@@ -122,6 +123,22 @@
                 pltpu.make_async_remote_copy(
                     modes.at[p, :, 0, pl.ds(pl.multiple_of(8 * (2 * other + lax.div(f, 4)), 8), 8), :], arrived.at[p, slot],
                     send_sem.at[0], mode_sem.at[p], device_id=device_at(p, f, other), device_id_type=MESH).start()
+
+    def plane_copies(piece):
+        rows = pl.ds(sum(PIECES[:piece]), PIECES[piece])
+        return [pltpu.make_async_remote_copy(
+            scalar.at[0, rows], planes.at[i, rows], send_sem.at[15 + 2 * piece + i], plane_sem.at[2 * piece + i],
+            device_id=(lax.rem(sec + step, SECS), row, col), device_id_type=MESH) for i, step in enumerate((1, 3))]
+
+    has_above, has_below = sec < SECS - 1, sec > 0
+
+    def send_planes(piece):
+        if PIECES[piece]:
+            up, down = plane_copies(piece)
+            pl.when(has_above)(up.start)
+            pl.when(has_below)(down.start)
+
+    send_planes(0)
 
     loads[1].wait()
     edges_out[0] = padded[pl.ds(8, 256), pl.ds(128, 128)].T[120:128]
@@ -150,55 +167,38 @@
         load.wait()
     pl.semaphore_wait(ready_sem, 3)
 
+    @pl.when(sec == 0)
+    def _():
+        planes[0] = jnp.zeros((256, 256), F32)
+
+    @pl.when(sec == SECS - 1)
+    def _():
+        planes[1] = jnp.zeros((256, 256), F32)
+
     def send_zero(p):
         return pltpu.make_async_remote_copy(
             row_zero.at[p], extra.at[p, lead[p]], send_sem.at[11 + p], extra_sem.at[p],
             device_id=device_at(p, lax.rem(8 - follow[p], 4), 0), device_id_type=MESH)
 
-    for p in (0, 2, 1):
+    for p in ORDER:
         pl.when(follow[p] >= 4)(send_zero(p).start)
     first = (row == 0) & (col == 0)
     sublane = lax.broadcasted_iota(jnp.int32, (8, 128), 0)
     special = sublane < jnp.where(first, 1, 0)
 
-    def owner_of(p, block, half):
+    def owners_of(p, block, half):
         if p < 2:
-            return (sec, 2 * (2 * p + half) + lax.rem(block, 2), block)
-        return (sec, block, 4 * half + 1 + lax.rem(block, 2))
-
-    parity = lax.rem(row + col, 2)
+            return [(sec, 2 * (2 * p + half) + lax.rem(lax.div(block, 2), 2), block)]
+        return [(sec, block, 4 * half + 2 * (1 - lax.rem(block, 2)) + side) for side in range(2)]
+
+    plain_owner = lax.rem(row + lax.div(col, 2), 2) == 0
     chunk = lax.div(row, 2)
-    plain_owner = parity == 0
-    turned_owner = lax.rem(col, 4) == 1 + lax.rem(row, 2)
     own_half = jnp.where(plain_owner, lax.rem(chunk, 2), lax.div(col, 4))
-    own_part = jnp.where(plain_owner, lax.div(chunk, 2), jnp.where(turned_owner, 2, 3))
-
-    def plane_copies(piece):
-        rows = pl.ds(0, EARLY) if piece == 0 else pl.ds(EARLY, 256 - EARLY)
-        return [pltpu.make_async_remote_copy(
-            scalar.at[0, rows], planes.at[i, rows], send_sem.at[7 + 2 * piece + i], plane_sem.at[2 * piece + i],
-            device_id=(lax.rem(sec + step, SECS), row, col), device_id_type=MESH) for i, step in enumerate((1, 3))]
-
-    has_above, has_below = sec < SECS - 1, sec > 0
-
-    def send_planes(piece):
-        up, down = plane_copies(piece)
-        pl.when(has_above)(up.start)
-        pl.when(has_below)(down.start)
-
-    @pl.when(sec == 0)
-    def _():
-        planes[0] = jnp.zeros((256, 256), F32)
-
-    @pl.when(sec == SECS - 1)
-    def _():
-        planes[1] = jnp.zeros((256, 256), F32)
-
-    for p in (0, 2, 1):
+    own_part = jnp.where(plain_owner, lax.div(chunk, 2), 2)
+
+    for p in ORDER:
         some = arrived.at[p, pl.ds(0, 15)]
         pltpu.make_async_copy(some, some, mode_sem.at[p]).wait()
-        if p == 0:
-            send_planes(0)
 
         @pl.when((lead[p] == 0) & (follow[p] < 4))
         def _():
@@ -236,22 +236,26 @@
         for i in range(8):
             block = lax.rem(lead[p] + i, 8)
             for half in range(2):
-                target = owner_of(p, block, half)
-                mine = target[1 if p < 2 else 2] == follow[p]
-
-                def away():
-                    pltpu.make_async_remote_copy(
-                        sent.at[p, block, half], spectra.at[:, rows, :], send_sem.at[1], spectra_sem,
-                        device_id=target, device_id_type=MESH).start()
-
-                if i > 0:
-                    away()
-                else:
-                    pl.when(jnp.logical_not(mine))(away)
-
-                    @pl.when(mine)
-                    def _():
-                        spectra[:, rows, :] = sent[p, block, half]
+                for target in owners_of(p, block, half):
+                    mine = target[1 if p < 2 else 2] == follow[p]
+
+                    def away():
+                        pltpu.make_async_remote_copy(
+                            sent.at[p, block, half], spectra.at[:, rows, :], send_sem.at[1], spectra_sem,
+                            device_id=target, device_id_type=MESH).start()
+
+                    if i > 0:
+                        away()
+                    else:
+                        pl.when(jnp.logical_not(mine))(away)
+
+                        @pl.when(mine)
+                        def _():
+                            spectra[:, rows, :] = sent[p, block, half]
+
+        if p == ORDER[0]:
+            send_planes(1)
+    send_planes(2)
 
     @pl.when(first)
     def _():
@@ -265,19 +269,23 @@
         high, low = split(lone[...])
         total = (jnp.dot(high, x_high[...], preferred_element_type=F32) + jnp.dot(low, x_high[...], preferred_element_type=F32)
                  + jnp.dot(high, x_low[...], preferred_element_type=F32))
-        for p in range(3):
-            for block in range(8):
-                for half in range(2):
-                    tile = jnp.broadcast_to(total[8 * p + block:8 * p + block + 1, 128 * half:128 * half + 128], (8, 128))
-                    if p == block == half == 0:
-                        lone_row[...] = tile
-                        continue
-                    index = (p * 8 + block) * 2 + half
-                    lone_sent[index] = tile
-                    pltpu.make_async_remote_copy(
-                        lone_sent.at[index], lone_row, send_sem.at[14], lone_sem,
-                        device_id=(sec, 2 * (2 * p + half) + block % 2, block) if p < 2 else (sec, block, 4 * half + 1 + block % 2),
-                        device_id_type=MESH).start()
+        def lone_tile(parts, block):
+            strip = [total[8 * p + block:8 * p + block + 1, 128 * half:128 * half + 128] for p in parts for half in range(2)]
+            blank = jnp.zeros((1, 128), F32)
+            strip = strip + [blank] * 4 if len(parts) == 2 else [blank] * 4 + strip + [blank] * 2
+            return jnp.concatenate(strip, 0)
+
+        by_col = [lone_tile((0, 1), c) for c in range(8)]
+        for r in range(8):
+            by_row = lone_tile((2,), r)
+            for c in range(8):
+                if r == c == 0:
+                    lone_row[...] = by_col[c] + by_row
+                    continue
+                lone_sent[8 * r + c] = by_col[c] + by_row
+                pltpu.make_async_remote_copy(
+                    lone_sent.at[8 * r + c], lone_row, send_sem.at[14], lone_sem,
+                    device_id=(sec, r, c), device_id_type=MESH).start()
 
     for copy in halo_copies:
         copy.wait()
@@ -297,71 +305,51 @@
         slopes[1, rows, :] = front - back
         base[rows, :] = here + 0.04 * (left + right + back + front - 6.0 * here) - 0.25 * flag * (here - 1.0)
 
-    @pl.when(own_part < 3)
-    def _():
-        pltpu.make_async_copy(spectra.at[:, pl.ds(0, 504), :], spectra.at[:, pl.ds(0, 504), :], spectra_sem).wait()
-        send_planes(1)
-
-        @pl.when(plain_owner)
-        def _():
-            pl.semaphore_signal(go_sem, inc=1, device_id=(sec, row + 1 - 2 * lax.rem(row, 2), col), device_id_type=MESH)
-
+    pltpu.make_async_copy(spectra.at[:, pl.ds(0, 504), :], spectra.at[:, pl.ds(0, 504), :], spectra_sem).wait()
+    send_planes(3)
+    for q in range(8):
+        for part in range(2):
+            high, low = split(spectra[part, pl.ds(q, 64, stride=8), :])
+            rhs[pl.ds(64 * part, 64), pl.ds(128 * q, 128)] = high
+            rhs[pl.ds(128 + 64 * part, 64), pl.ds(128 * q, 128)] = low
+    waves[...] = (jnp.dot(y_high[...], rhs[...], preferred_element_type=F32)
+                  + jnp.dot(y_low[...], rhs[pl.ds(0, 128), :], preferred_element_type=F32))
+
+    quarter = lax.rem(lax.broadcasted_iota(jnp.int32, (16, 128), 0), 4)
+    lone_real = jnp.where(quarter == 0, 1.0, jnp.where(quarter == 2, -1.0, 0.0)) * spectra[1, 0:1, :]
+
+    def combine(i, carry):
+        at = pl.multiple_of(16 * i, 16)
+        rows = pl.ds(at, 16)
+        real, imag = [], []
         for q in range(8):
-            for part in range(2):
-                high, low = split(spectra[part, pl.ds(q, 64, stride=8), :])
-                rhs[pl.ds(64 * part, 64), pl.ds(128 * q, 128)] = high
-                rhs[pl.ds(128 + 64 * part, 64), pl.ds(128 * q, 128)] = low
-        waves[...] = (jnp.dot(y_high[...], rhs[...], preferred_element_type=F32)
-                      + jnp.dot(y_low[...], rhs[pl.ds(0, 128), :], preferred_element_type=F32))
-
-        @pl.when(jnp.logical_not(first))
-        def _():
-            pltpu.make_async_copy(lone_row, lone_row, lone_sem).wait()
-
-        quarter = lax.rem(lax.broadcasted_iota(jnp.int32, (16, 128), 0), 4)
-        lone_term = (jnp.where(quarter == 0, 1.0, jnp.where(quarter == 2, -1.0, 0.0)) * spectra[1, 0:1, :]
-                     + jnp.where(quarter == 1, 1.0, jnp.where(quarter == 3, -1.0, 0.0)) * lone_row[0:1, :])
-
-        def combine(i, carry):
-            at = pl.multiple_of(16 * i, 16)
-            rows = pl.ds(at, 16)
-            real, imag = [], []
-            for q in range(8):
-                re = waves[rows, pl.ds(128 * q, 128)]
-                if q == 0:
-                    real.append(re + lone_term)
-                    imag.append(None)
-                    continue
-                im = waves[pl.ds(256 + at, 16), pl.ds(128 * q, 128)]
-                cosine, sine = twist[0, q - 1, rows, :], twist[1, q - 1, rows, :]
-                real.append(re * cosine - im * sine)
-                imag.append(None if q == 4 else re * sine + im * cosine)
-            a1, b1 = real[1] + real[7], imag[1] - imag[7]
-            a2, b2 = real[2] + real[6], imag[2] - imag[6]
-            a3, b3 = real[3] + real[5], imag[3] - imag[5]
-            even, odd = real[0] + real[4], real[0] - real[4]
-            e0, e2, e1, e3 = even + a2, even - a2, odd - b2, odd + b2
-            d0, d2 = a1 + a3, b3 - b1
-            amid, bmid = HALF_ROOT * (a1 - a3), HALF_ROOT * (b1 + b3)
-            d1, d3 = amid - bmid, -amid - bmid
-            for r, (e, d) in enumerate(((e0, d0), (e1, d1), (e2, d2), (e3, d3))):
-                fields[r, rows, :] = e + d
-                fields[r + 4, rows, :] = e - d
-            return carry
-
-        lax.fori_loop(0, 16, combine, 0)
-
-    @pl.when(parity == 1)
-    def _():
-        pl.semaphore_wait(go_sem, 1)
-
-    @pl.when(own_part == 3)
-    def _():
-        send_planes(1)
-
-    def send_fields(number, peers):
+            re = waves[rows, pl.ds(128 * q, 128)]
+            if q == 0:
+                real.append(re + lone_real)
+                imag.append(None)
+                continue
+            im = waves[pl.ds(256 + at, 16), pl.ds(128 * q, 128)]
+            cosine, sine = twist[0, q - 1, rows, :], twist[1, q - 1, rows, :]
+            real.append(re * cosine - im * sine)
+            imag.append(None if q == 4 else re * sine + im * cosine)
+        a1, b1 = real[1] + real[7], imag[1] - imag[7]
+        a2, b2 = real[2] + real[6], imag[2] - imag[6]
+        a3, b3 = real[3] + real[5], imag[3] - imag[5]
+        even, odd = real[0] + real[4], real[0] - real[4]
+        e0, e2, e1, e3 = even + a2, even - a2, odd - b2, odd + b2
+        d0, d2 = a1 + a3, b3 - b1
+        amid, bmid = HALF_ROOT * (a1 - a3), HALF_ROOT * (b1 + b3)
+        d1, d3 = amid - bmid, -amid - bmid
+        for r, (e, d) in enumerate(((e0, d0), (e1, d1), (e2, d2), (e3, d3))):
+            fields[r, rows, :] = e + d
+            fields[r + 4, rows, :] = e - d
+        return carry
+
+    lax.fori_loop(0, 16, combine, 0)
+
+    def send_fields(number, peers, steps):
         def go():
-            for i in range(1, 8):
+            for i in steps:
                 peer = lax.rem(number + i, 8)
                 pltpu.make_async_remote_copy(
                     fields.at[peer], velocity.at[own_part, own_half], send_sem.at[2], velocity_sem.at[own_part],
@@ -369,10 +357,11 @@
             velocity[own_part, own_half] = fields[number]
         return go
 
-    pl.when(own_part < 2)(send_fields(row, at_row))
-    pl.when(own_part == 2)(send_fields(col, at_col))
-
-    for piece in range(2):
+    pl.when(plain_owner)(send_fields(row, at_row, range(1, 8)))
+    pl.when(jnp.logical_not(plain_owner))(send_fields(col, at_col, (2, 4, 6)))
+
+    pieces = [piece for piece in range(4) if PIECES[piece]]
+    for piece in pieces:
         up, down = plane_copies(piece)
         pl.when(has_below)(up.wait_recv)
         pl.when(has_above)(down.wait_recv)
@@ -384,39 +373,47 @@
         two = pltpu.make_async_copy(velocity.at[p], velocity.at[p], velocity_sem.at[p])
         pl.when(own_part == p)(one.wait)
         pl.when(own_part != p)(two.wait)
-    for half in range(2):
-        rows = pl.ds(128 * half, 128)
-        turned = velocity[2, half].T
-        for block in range(2):
-            lanes = pl.ds(128 * block, 128)
+    @pl.when(jnp.logical_not(first))
+    def _():
+        pltpu.make_async_copy(lone_row, lone_row, lone_sem).wait()
+
+    quarter = lax.rem(lax.broadcasted_iota(jnp.int32, (256, 128), 0), 4)
+    swing = jnp.where(quarter == 1, 1.0, jnp.where(quarter == 3, -1.0, 0.0))
+
+    def field(p, half):
+        return velocity[p, half] + swing * lone_row[2 * p + half:2 * p + half + 1, :]
+
+    turned = [field(2, half).T for half in range(2)]
+    for block in range(2):
+        lanes = pl.ds(128 * block, 128)
+        partial = field(0, block) * slopes[0, :, lanes] + field(1, block) * slopes[1, :, lanes]
+        for half in range(2):
+            rows = pl.ds(128 * half, 128)
             out[0, rows, lanes] = base[rows, lanes] - 0.125 * (
-                velocity[0, block, rows, :] * slopes[0, rows, lanes] + velocity[1, block, rows, :] * slopes[1, rows, lanes]
-                + turned[:, 128 * block:128 * block + 128] * slopes[2, rows, lanes])
+                partial[128 * half:128 * half + 128] + turned[half][:, 128 * block:128 * block + 128] * slopes[2, rows, lanes])
 
     sent_modes = arrived.at[:, pl.ds(0, 15)]
     pltpu.make_async_copy(sent_modes, sent_modes, send_sem.at[0]).wait()
 
-    @pl.when(own_part < 3)
-    def _():
-        some = spectra.at[:, pl.ds(0, 47 * 8), :]
-        pltpu.make_async_copy(some, some, send_sem.at[1]).wait()
-        most = fields.at[pl.ds(0, 7)]
-        pltpu.make_async_copy(most, most, send_sem.at[2]).wait()
-
-    @pl.when(own_part == 3)
-    def _():
-        some = spectra.at[:, pl.ds(0, 48 * 8), :]
-        pltpu.make_async_copy(some, some, send_sem.at[1]).wait()
+    some = spectra.at[:, pl.ds(0, 63 * 8), :]
+    pltpu.make_async_copy(some, some, send_sem.at[1]).wait()
+
+    def fields_left(count):
+        most = fields.at[pl.ds(0, count)]
+        return pltpu.make_async_copy(most, most, send_sem.at[2]).wait
+
+    pl.when(plain_owner)(fields_left(7))
+    pl.when(jnp.logical_not(plain_owner))(fields_left(3))
 
     for p in range(3):
         pl.when(follow[p] >= 4)(send_zero(p).wait_send)
 
     @pl.when(first)
     def _():
-        some = lone_sent.at[pl.ds(1, 47)]
+        some = lone_sent.at[pl.ds(1, 63)]
         pltpu.make_async_copy(some, some, send_sem.at[14]).wait()
 
-    for piece in range(2):
+    for piece in pieces:
         up, down = plane_copies(piece)
         pl.when(has_above)(up.wait_send)
         pl.when(has_below)(down.wait_send)
@@ -430,7 +427,7 @@
     dma = pltpu.SemaphoreType.DMA
     return pl.pallas_call(
         kernel,
-        out_shape=jax.ShapeDtypeStruct((1, 256, 256), F32),
+        out_shape=pltpu.VMEM((1, 256, 256), F32),
         in_specs=[anywhere, anywhere, smem] + [anywhere] * 6,
         out_specs=vmem,
         scratch_shapes=[
@@ -446,7 +443,7 @@
             pltpu.VMEM((256, 16), F32),
             pltpu.VMEM((256, 2048), BF16),
             pltpu.VMEM((32, 2048), F32),
-            pltpu.VMEM((48, 8, 128), F32),
+            pltpu.VMEM((64, 8, 128), F32),
             pltpu.VMEM((8, 128), F32),
             pltpu.VMEM((3, 8, 2, 2, 8, 128), F32),
             pltpu.VMEM((2, 512, 128), F32),
@@ -461,7 +458,7 @@
             pltpu.VMEM((2, 256, 256), F32),
             pltpu.VMEM((256, 256), F32),
             pltpu.VMEM((3, 256, 256), F32),
-            dma((8,)), dma((3,)), dma((3,)), dma, dma, dma((3,)), dma((4,)), dma((4,)), dma((15,)), pltpu.SemaphoreType.REGULAR, pltpu.SemaphoreType.REGULAR,
+            dma((8,)), dma((3,)), dma((3,)), dma, dma, dma((3,)), dma((4,)), dma((8,)), dma((23,)), pltpu.SemaphoreType.REGULAR,
         ],
         compiler_params=pltpu.CompilerParams(
             collective_id=0, has_side_effects=True, vmem_limit_bytes=56 * 1024 * 1024),

time: 42.2 us -> 37.7 us (0.89)
  the two profiles are of different devices: /device:TPU:70 before, /device:TPU:1 now
where the time goes in v4:
time: 37.7 us; the launch traced here: 37 us
  Pallas kernels  36.3 us (96%)
  local copies, waits for them, and re-layouts  0.71 us (2%)
    pallas_call x1, Pallas kernels, body(): pl.pallas_call(kernel, out_shape=pltpu.VMEM((1, 256, 256), F32), in_specs...  36.3 us

profile of v4, /device:TPU:1, one launch (start us, length us, event | category | flops | bytes accessed | tf_op | source)
XLA Modules:
  0.0 37.0 jit_solution(7565872065299758648)
XLA Ops:
  0.0 36.3 %shard_map.91 = f32[1,256,256]{2,1,0:T(8,128)S(1)} custom-call(f32[3,2,1,128,128]{4,3,2,1,0:T(8,128)} %modes_in.1, f32[1,256,256]{2,1,0:T(8,128)} %scalar.1, s32[1,2,2]{2,1,0:T(2,128)} %obstacle.1, bf16[2048,256]{1,0:T(8,128)(2,1)} %constant.12.clone.x_high_in, bf16[2048,256]{1,0:T(8,128)(2,1)} %constant.13.clone.x_low_in, ...), custom_call_target="tpu_custom_call" | custom-call | tf_op jit(solution)/shard_map/pallas_call | solution.py:428
  36.3 0.7 %copy.11 = f32[1,256,256]{2,1,0:T(8,128)} copy(f32[1,256,256]{2,1,0:T(8,128)S(1)} %shard_map.91) | data formatting | bytes 524288

commit v5 on v4

--- a/solution.py
+++ b/solution.py
@@ -13,7 +13,8 @@
 ROWS = 8
 COLS = 8
 SECS = 4
-PIECES = (0,64,0,192)
+FAR_FIRST = (4, 5, 3, 2, 6, 1, 7)
+PIECES = (48,0,32,176)
 ORDER = (0,1,2)
 F32 = jnp.float32
 BF16 = jnp.bfloat16
@@ -66,26 +67,44 @@
            table_sem, mode_sem, extra_sem, lone_sem, spectra_sem, velocity_sem, halo_sem, plane_sem, send_sem, ready_sem):
     sec, row, col = lax.axis_index("sec"), lax.axis_index("row"), lax.axis_index("col")
 
+    barrier = pltpu.get_barrier_semaphore()
+
+    def at_row(i):
+        return (sec, lax.rem(row + i, ROWS), col)
+
+    def at_col(i):
+        return (sec, row, lax.rem(col + i, COLS))
+
+    greeted = [(sec, 7 - row, lax.rem(col + i, COLS)) for i in FAR_FIRST + (0,)]
+    greeted += [(sec, flip(row, i), c) for c in (7 - col, col) for i in range(6, 0, -1)]
+    greeted += [at_col(i) for i in FAR_FIRST]
+    for device in greeted:
+        pl.semaphore_signal(barrier, inc=1, device_id=device, device_id_type=MESH)
+    @pl.when((col == 0) & (row < 4))
+    def _():
+        for i in range(8):
+            pl.semaphore_signal(barrier, inc=1, device_id=(sec, jnp.where(row > 0, 8 - row, 4), i), device_id_type=MESH)
+
+    @pl.when((row == 0) & (col < 4))
+    def _():
+        for i in range(8):
+            pl.semaphore_signal(barrier, inc=1, device_id=(sec, i, jnp.where(col > 0, 8 - col, 4)), device_id_type=MESH)
+
+    has_above, has_below = sec < SECS - 1, sec > 0
+
+    @pl.when(has_above)
+    def _():
+        pl.semaphore_signal(barrier, inc=1, device_id=(lax.rem(sec + 1, SECS), row, col), device_id_type=MESH)
+
+    @pl.when(has_below)
+    def _():
+        pl.semaphore_signal(barrier, inc=1, device_id=(lax.rem(sec + SECS - 1, SECS), row, col), device_id_type=MESH)
+
     pairs = ((modes_in, modes), (scalar.at[0], padded.at[pl.ds(8, 256)]), (twiddles_in, twiddles), (phases_in, phases),
              (x_high_in, x_high), (x_low_in, x_low), (y_high_in, y_high), (y_low_in, y_low))
     loads = [pltpu.make_async_copy(here, there, table_sem.at[i]) for i, (here, there) in enumerate(pairs)]
     for load in loads:
         load.start()
-
-    barrier = pltpu.get_barrier_semaphore()
-
-    def at_row(i):
-        return (sec, lax.rem(row + i, ROWS), col)
-
-    def at_col(i):
-        return (sec, row, lax.rem(col + i, COLS))
-
-    greeted = [at_col(i) for i in range(1, 8)] + [(sec, 7 - row, lax.rem(col + i, COLS)) for i in range(8)]
-    greeted += [(sec, flip(row, i), c) for i in range(1, 7) for c in (col, 7 - col)]
-    for device in greeted:
-        pl.semaphore_signal(barrier, inc=1, device_id=device, device_id_type=MESH)
-    for step in (1, 3):
-        pl.semaphore_signal(barrier, inc=1, device_id=(lax.rem(sec + step, SECS), row, col), device_id_type=MESH)
 
     lead = (col, col, row)
     follow = (row, row, col)
@@ -111,13 +130,21 @@
 
     for p in ORDER:
         pl.when(follow[p] >= 4)(turn_round(p))
-    pl.semaphore_wait(barrier, 29)
+    pl.semaphore_wait(barrier, 28 + lax.rem(lax.div(sec + 1, 2), 2) + lax.div(row, 4) + lax.div(col, 4))
     for i in (1, 2, 3):
         pl.semaphore_signal(ready_sem, inc=1, device_id=(sec, flip(row, i), col), device_id_type=MESH)
 
+    def send_zero(p):
+        return pltpu.make_async_remote_copy(
+            row_zero.at[p], extra.at[p, lead[p]], send_sem.at[11 + p], extra_sem.at[p],
+            device_id=device_at(p, lax.rem(8 - follow[p], 4), 0), device_id_type=MESH)
+
+    for p in ORDER:
+        pl.when(follow[p] >= 4)(send_zero(p).start)
+
     for p in ORDER:
         slot = 8 * upper[p] + lead[p]
-        for i in range(8):
+        for i in FAR_FIRST + (0,):
             other = lax.rem(lead[p] + i, 8)
             for f in ((follow[p], 7 - follow[p]) if i else (7 - follow[p],)):
                 pltpu.make_async_remote_copy(
@@ -130,15 +157,11 @@
             scalar.at[0, rows], planes.at[i, rows], send_sem.at[15 + 2 * piece + i], plane_sem.at[2 * piece + i],
             device_id=(lax.rem(sec + step, SECS), row, col), device_id_type=MESH) for i, step in enumerate((1, 3))]
 
-    has_above, has_below = sec < SECS - 1, sec > 0
-
     def send_planes(piece):
         if PIECES[piece]:
             up, down = plane_copies(piece)
             pl.when(has_above)(up.start)
             pl.when(has_below)(down.start)
-
-    send_planes(0)
 
     loads[1].wait()
     edges_out[0] = padded[pl.ds(8, 256), pl.ds(128, 128)].T[120:128]
@@ -175,13 +198,6 @@
     def _():
         planes[1] = jnp.zeros((256, 256), F32)
 
-    def send_zero(p):
-        return pltpu.make_async_remote_copy(
-            row_zero.at[p], extra.at[p, lead[p]], send_sem.at[11 + p], extra_sem.at[p],
-            device_id=device_at(p, lax.rem(8 - follow[p], 4), 0), device_id_type=MESH)
-
-    for p in ORDER:
-        pl.when(follow[p] >= 4)(send_zero(p).start)
     first = (row == 0) & (col == 0)
     sublane = lax.broadcasted_iota(jnp.int32, (8, 128), 0)
     special = sublane < jnp.where(first, 1, 0)
@@ -195,6 +211,10 @@
     chunk = lax.div(row, 2)
     own_half = jnp.where(plain_owner, lax.rem(chunk, 2), lax.div(col, 4))
     own_part = jnp.where(plain_owner, lax.div(chunk, 2), 2)
+
+    sent_modes = arrived.at[:, pl.ds(0, 15)]
+    pltpu.make_async_copy(sent_modes, sent_modes, send_sem.at[0]).wait()
+    send_planes(0)
 
     for p in ORDER:
         some = arrived.at[p, pl.ds(0, 15)]
@@ -233,7 +253,7 @@
                 sent[p, block, half, 1] = tile[8:]
 
         rows = pl.ds(pl.multiple_of(8 * (16 * group[p] + 2 * lead[p] + upper[p]), 8), 8)
-        for i in range(8):
+        for i in FAR_FIRST + (0,):
             block = lax.rem(lead[p] + i, 8)
             for half in range(2):
                 for target in owners_of(p, block, half):
@@ -255,7 +275,8 @@
 
         if p == ORDER[0]:
             send_planes(1)
-    send_planes(2)
+        elif p == ORDER[1]:
+            send_planes(2)
 
     @pl.when(first)
     def _():
@@ -357,8 +378,8 @@
             velocity[own_part, own_half] = fields[number]
         return go
 
-    pl.when(plain_owner)(send_fields(row, at_row, range(1, 8)))
-    pl.when(jnp.logical_not(plain_owner))(send_fields(col, at_col, (2, 4, 6)))
+    pl.when(plain_owner)(send_fields(row, at_row, FAR_FIRST))
+    pl.when(jnp.logical_not(plain_owner))(send_fields(col, at_col, (4, 2, 6)))
 
     pieces = [piece for piece in range(4) if PIECES[piece]]
     for piece in pieces:
@@ -392,8 +413,6 @@
             out[0, rows, lanes] = base[rows, lanes] - 0.125 * (
                 partial[128 * half:128 * half + 128] + turned[half][:, 128 * block:128 * block + 128] * slopes[2, rows, lanes])
 
-    sent_modes = arrived.at[:, pl.ds(0, 15)]
-    pltpu.make_async_copy(sent_modes, sent_modes, send_sem.at[0]).wait()
 
     some = spectra.at[:, pl.ds(0, 63 * 8), :]
     pltpu.make_async_copy(some, some, send_sem.at[1]).wait()

time: 37.7 us -> 36.6 us (0.971)
  the two profiles are of different devices: /device:TPU:1 before, /device:TPU:65 now
where the time goes in v5:
time: 36.6 us; the launch traced here: 36.5 us
  Pallas kernels  35.8 us (98%)
  local copies, waits for them, and re-layouts  0.71 us (2%)
    pallas_call x1, Pallas kernels, body(): pl.pallas_call(kernel, out_shape=pltpu.VMEM((1, 256, 256), F32), in_specs...  35.8 us

profile of v5, /device:TPU:65, one launch (start us, length us, event | category | flops | bytes accessed | tf_op | source)
XLA Modules:
  0.0 36.5 jit_solution(16428989039229083753)
XLA Ops:
  0.0 35.8 %shard_map.91 = f32[1,256,256]{2,1,0:T(8,128)S(1)} custom-call(f32[3,2,1,128,128]{4,3,2,1,0:T(8,128)} %modes_in.1, f32[1,256,256]{2,1,0:T(8,128)} %scalar.1, s32[1,2,2]{2,1,0:T(2,128)} %obstacle.1, bf16[2048,256]{1,0:T(8,128)(2,1)} %constant.12.clone.x_high_in, bf16[2048,256]{1,0:T(8,128)(2,1)} %constant.13.clone.x_low_in, ...), custom_call_target="tpu_custom_call" | custom-call | tf_op jit(solution)/shard_map/pallas_call | solution.py:447
  35.8 0.7 %copy.11 = f32[1,256,256]{2,1,0:T(8,128)} copy(f32[1,256,256]{2,1,0:T(8,128)S(1)} %shard_map.91) | data formatting | bytes 524288

commit v6 on v5

--- a/solution.py
+++ b/solution.py
@@ -14,7 +14,7 @@
 COLS = 8
 SECS = 4
 FAR_FIRST = (4, 5, 3, 2, 6, 1, 7)
-PIECES = (48,0,32,176)
+PIECES = (32,32,64,128)
 ORDER = (0,1,2)
 F32 = jnp.float32
 BF16 = jnp.bfloat16
@@ -62,9 +62,9 @@
 
 
 def kernel(modes_in, scalar, obstacle, x_high_in, x_low_in, y_high_in, y_low_in, phases_in, twiddles_in, out,
-           modes, row_zero, extra, arrived, x_high, x_low, y_high, y_low, phases, twiddles, lhs, lone, lone_sent, lone_row, sent, spectra, rhs, waves, twist, fields, velocity,
+           modes, row_zero, extra, arrived, twice, x_high, x_low, y_high, y_low, phases, twiddles, lhs, lone, lone_sent, lone_row, sent, sent_twice, spectra, rhs, waves, twist, fields, velocity,
            padded, edges_out, edges_in, planes, base, slopes,
-           table_sem, mode_sem, extra_sem, lone_sem, spectra_sem, velocity_sem, halo_sem, plane_sem, send_sem, ready_sem):
+           table_sem, mode_sem, extra_sem, lone_sem, spectra_sem, velocity_sem, halo_sem, plane_sem, send_sem, ready_sem, above_sem):
     sec, row, col = lax.axis_index("sec"), lax.axis_index("row"), lax.axis_index("col")
 
     barrier = pltpu.get_barrier_semaphore()
@@ -85,20 +85,17 @@
         for i in range(8):
             pl.semaphore_signal(barrier, inc=1, device_id=(sec, jnp.where(row > 0, 8 - row, 4), i), device_id_type=MESH)
 
-    @pl.when((row == 0) & (col < 4))
-    def _():
+    @pl.when(row == 0)
+    def _():
+        source = jnp.where(col < 4, jnp.where(col > 0, 8 - col, 4), jnp.where(col < 7, col + 1, 4))
         for i in range(8):
-            pl.semaphore_signal(barrier, inc=1, device_id=(sec, i, jnp.where(col > 0, 8 - col, 4)), device_id_type=MESH)
+            pl.semaphore_signal(barrier, inc=1, device_id=(sec, i, source), device_id_type=MESH)
 
     has_above, has_below = sec < SECS - 1, sec > 0
 
     @pl.when(has_above)
     def _():
         pl.semaphore_signal(barrier, inc=1, device_id=(lax.rem(sec + 1, SECS), row, col), device_id_type=MESH)
-
-    @pl.when(has_below)
-    def _():
-        pl.semaphore_signal(barrier, inc=1, device_id=(lax.rem(sec + SECS - 1, SECS), row, col), device_id_type=MESH)
 
     pairs = ((modes_in, modes), (scalar.at[0], padded.at[pl.ds(8, 256)]), (twiddles_in, twiddles), (phases_in, phases),
              (x_high_in, x_high), (x_low_in, x_low), (y_high_in, y_high), (y_low_in, y_low))
@@ -130,17 +127,24 @@
 
     for p in ORDER:
         pl.when(follow[p] >= 4)(turn_round(p))
-    pl.semaphore_wait(barrier, 28 + lax.rem(lax.div(sec + 1, 2), 2) + lax.div(row, 4) + lax.div(col, 4))
+    pl.semaphore_wait(barrier, 27 + lax.div(sec + 3, 4) + lax.div(row, 4) + 2 * lax.div(col, 4))
+
+    @pl.when(has_below)
+    def _():
+        pl.semaphore_signal(above_sem, inc=1, device_id=(lax.rem(sec + SECS - 1, SECS), row, col), device_id_type=MESH)
+
     for i in (1, 2, 3):
         pl.semaphore_signal(ready_sem, inc=1, device_id=(sec, flip(row, i), col), device_id_type=MESH)
 
-    def send_zero(p):
+    def send_zero(p, copy=0):
+        target = lax.rem(8 - follow[p], 4)
         return pltpu.make_async_remote_copy(
-            row_zero.at[p], extra.at[p, lead[p]], send_sem.at[11 + p], extra_sem.at[p],
-            device_id=device_at(p, lax.rem(8 - follow[p], 4), 0), device_id_type=MESH)
-
-    for p in ORDER:
-        pl.when(follow[p] >= 4)(send_zero(p).start)
+            row_zero.at[p], extra.at[p, lead[p]], send_sem.at[11 + p if copy == 0 else 23], extra_sem.at[p],
+            device_id=device_at(p, target if copy == 0 else 7 - target, 0), device_id_type=MESH)
+
+    zero_copies = ((0, 0), (1, 0), (2, 0), (2, 1))
+    for p, copy in zero_copies:
+        pl.when(follow[p] >= 4)(send_zero(p, copy).start)
 
     for p in ORDER:
         slot = 8 * upper[p] + lead[p]
@@ -148,7 +152,9 @@
             other = lax.rem(lead[p] + i, 8)
             for f in ((follow[p], 7 - follow[p]) if i else (7 - follow[p],)):
                 pltpu.make_async_remote_copy(
-                    modes.at[p, :, 0, pl.ds(pl.multiple_of(8 * (2 * other + lax.div(f, 4)), 8), 8), :], arrived.at[p, slot],
+                    modes.at[p, :, 0, pl.ds(pl.multiple_of(8 * (2 * other + lax.div(f, 4)), 8), 8), :] if p < 2
+                    else modes.at[p, :, 0, pl.ds(pl.multiple_of(16 * other, 16), 16), :],
+                    arrived.at[p, slot] if p < 2 else twice.at[slot],
                     send_sem.at[0], mode_sem.at[p], device_id=device_at(p, f, other), device_id_type=MESH).start()
 
     def plane_copies(piece):
@@ -183,7 +189,8 @@
     for q in range(1, 8):
         twist[0, q - 1] = jnp.broadcast_to(twiddles[:, q:q + 1], (256, 128))
         twist[1, q - 1] = jnp.broadcast_to(twiddles[:, 8 + q:9 + q], (256, 128))
-    for p in range(3):
+    twice[8 * upper[2] + lead[2]] = modes[2, :, 0, pl.ds(pl.multiple_of(16 * lead[2], 16), 16), :]
+    for p in range(2):
         own = 2 * lead[p] + upper[p]
         arrived[p, 8 * upper[p] + lead[p]] = modes[p, :, 0, pl.ds(pl.multiple_of(8 * own, 8), 8), :]
     for load in loads[3:]:
@@ -199,36 +206,40 @@
         planes[1] = jnp.zeros((256, 256), F32)
 
     first = (row == 0) & (col == 0)
-    sublane = lax.broadcasted_iota(jnp.int32, (8, 128), 0)
-    special = sublane < jnp.where(first, 1, 0)
 
     def owners_of(p, block, half):
         if p < 2:
             return [(sec, 2 * (2 * p + half) + lax.rem(lax.div(block, 2), 2), block)]
-        return [(sec, block, 4 * half + 2 * (1 - lax.rem(block, 2)) + side) for side in range(2)]
+        return [(sec, block, 4 * half + 2 * (1 - lax.rem(block, 2)) + side) for side in (lax.rem(col, 2),)]
 
     plain_owner = lax.rem(row + lax.div(col, 2), 2) == 0
     chunk = lax.div(row, 2)
     own_half = jnp.where(plain_owner, lax.rem(chunk, 2), lax.div(col, 4))
     own_part = jnp.where(plain_owner, lax.div(chunk, 2), 2)
 
-    sent_modes = arrived.at[:, pl.ds(0, 15)]
-    pltpu.make_async_copy(sent_modes, sent_modes, send_sem.at[0]).wait()
-    send_planes(0)
+    @pl.when(has_above)
+    def _():
+        pl.semaphore_wait(above_sem, 1)
 
     for p in ORDER:
-        some = arrived.at[p, pl.ds(0, 15)]
+        size = 8 if p < 2 else 16
+        gathered = arrived.at[p] if p < 2 else twice
+        some = gathered.at[pl.ds(0, 15)]
         pltpu.make_async_copy(some, some, mode_sem.at[p]).wait()
-
-        @pl.when((lead[p] == 0) & (follow[p] < 4))
+        if p == ORDER[0]:
+            send_planes(0)
+
+        @pl.when((lead[p] == 0) & (follow[p] < (4 if p < 2 else 8)))
         def _():
             pltpu.make_async_copy(extra.at[p], extra.at[p], extra_sem.at[p]).wait()
             for a in range(8):
                 for part in range(2):
-                    arrived[p, 8 + a, part, 0:1] = jnp.where(follow[p] > 0, extra[p, a, part:part + 1], 0.0)
-
+                    gathered[8 + a, part, 0:1] = jnp.where(group[p] > 0, extra[p, a, part:part + 1], 0.0)
+
+        alone = jnp.where((lead[p] == 0) & (group[p] == 0) & (follow[p] < (4 if p < 2 else 8)), 1, 0)
+        special = lax.broadcasted_iota(jnp.int32, (size, 128), 0) < alone
         for a in range(8):
-            plus, minus = arrived[p, a], arrived[p, 8 + a]
+            plus, minus = gathered[a], gathered[8 + a]
             sum_real, sum_imag = plus[0] + minus[0], plus[1] + minus[1]
             gap_real = jnp.where(special, extra[p, a, 1:2], plus[0] - minus[0])
             gap_imag = jnp.where(special, -extra[p, a, 0:1], plus[1] - minus[1])
@@ -241,18 +252,20 @@
                     b_real, b_imag = gap_real * cosine - gap_imag * sine, gap_real * sine + gap_imag * cosine
                 for part, tile in enumerate(((a_real, -b_imag), (-a_imag, -b_real))):
                     high, low = split(jnp.concatenate(tile, 0))
-                    lhs[pl.ds(16 * block, 16), pl.ds(1024 * part + 128 * a, 128)] = high
-                    lhs[pl.ds(128 + 16 * block, 16), pl.ds(1024 * part + 128 * a, 128)] = low
-        main = jnp.dot(lhs[...], x_high[...], preferred_element_type=F32)
-        rest = jnp.dot(lhs[pl.ds(0, 128), :], x_low[...], preferred_element_type=F32)
-        total = main[:128] + main[128:] + rest
+                    lhs[pl.ds(2 * size * block, 2 * size), pl.ds(1024 * part + 128 * a, 128)] = high
+                    lhs[pl.ds(2 * size * (8 + block), 2 * size), pl.ds(1024 * part + 128 * a, 128)] = low
+        main = jnp.dot(lhs[pl.ds(0, 32 * size), :], x_high[...], preferred_element_type=F32)
+        rest = jnp.dot(lhs[pl.ds(0, 16 * size), :], x_low[...], preferred_element_type=F32)
+        total = main[:16 * size] + main[16 * size:] + rest
+        results = sent.at[p] if p < 2 else sent_twice
         for block in range(8):
             for half in range(2):
-                tile = total[16 * block:16 * block + 16, 128 * half:128 * half + 128]
-                sent[p, block, half, 0] = tile[:8]
-                sent[p, block, half, 1] = tile[8:]
-
-        rows = pl.ds(pl.multiple_of(8 * (16 * group[p] + 2 * lead[p] + upper[p]), 8), 8)
+                tile = total[2 * size * block:2 * size * (block + 1), 128 * half:128 * half + 128]
+                results[block, half, 0] = tile[:size]
+                results[block, half, 1] = tile[size:]
+
+        place = 128 * group[p] + (8 * (2 * lead[p] + upper[p]) if p < 2 else 16 * lead[p])
+        rows = pl.ds(pl.multiple_of(place, size), size)
         for i in FAR_FIRST + (0,):
             block = lax.rem(lead[p] + i, 8)
             for half in range(2):
@@ -261,7 +274,7 @@
 
                     def away():
                         pltpu.make_async_remote_copy(
-                            sent.at[p, block, half], spectra.at[:, rows, :], send_sem.at[1], spectra_sem,
+                            results.at[block, half], spectra.at[:, rows, :], send_sem.at[1], spectra_sem,
                             device_id=target, device_id_type=MESH).start()
 
                     if i > 0:
@@ -271,12 +284,11 @@
 
                         @pl.when(mine)
                         def _():
-                            spectra[:, rows, :] = sent[p, block, half]
+                            spectra[:, rows, :] = results[block, half]
 
         if p == ORDER[0]:
             send_planes(1)
-        elif p == ORDER[1]:
-            send_planes(2)
+    send_planes(2)
 
     @pl.when(first)
     def _():
@@ -326,7 +338,12 @@
         slopes[1, rows, :] = front - back
         base[rows, :] = here + 0.04 * (left + right + back + front - 6.0 * here) - 0.25 * flag * (here - 1.0)
 
-    pltpu.make_async_copy(spectra.at[:, pl.ds(0, 504), :], spectra.at[:, pl.ds(0, 504), :], spectra_sem).wait()
+    def spectra_through(semaphore):
+        for count, here in ((504, plain_owner), (496, jnp.logical_not(plain_owner))):
+            some = spectra.at[:, pl.ds(0, count), :]
+            pl.when(here)(pltpu.make_async_copy(some, some, semaphore).wait)
+
+    spectra_through(spectra_sem)
     send_planes(3)
     for q in range(8):
         for part in range(2):
@@ -413,9 +430,10 @@
             out[0, rows, lanes] = base[rows, lanes] - 0.125 * (
                 partial[128 * half:128 * half + 128] + turned[half][:, 128 * block:128 * block + 128] * slopes[2, rows, lanes])
 
-
-    some = spectra.at[:, pl.ds(0, 63 * 8), :]
-    pltpu.make_async_copy(some, some, send_sem.at[1]).wait()
+    sent_modes = spectra.at[:, pl.ds(0, 480), :]
+    pltpu.make_async_copy(sent_modes, sent_modes, send_sem.at[0]).wait()
+
+    spectra_through(send_sem.at[1])
 
     def fields_left(count):
         most = fields.at[pl.ds(0, count)]
@@ -424,8 +442,8 @@
     pl.when(plain_owner)(fields_left(7))
     pl.when(jnp.logical_not(plain_owner))(fields_left(3))
 
-    for p in range(3):
-        pl.when(follow[p] >= 4)(send_zero(p).wait_send)
+    for p, copy in zero_copies:
+        pl.when(follow[p] >= 4)(send_zero(p, copy).wait_send)
 
     @pl.when(first)
     def _():
@@ -453,18 +471,20 @@
             pltpu.VMEM((3, 2, 1, 128, 128), F32),
             pltpu.VMEM((3, 8, 128), F32),
             pltpu.VMEM((3, 8, 8, 128), F32),
-            pltpu.VMEM((3, 16, 2, 8, 128), F32),
+            pltpu.VMEM((2, 16, 2, 8, 128), F32),
+            pltpu.VMEM((16, 2, 16, 128), F32),
             pltpu.VMEM((2048, 256), BF16),
             pltpu.VMEM((2048, 256), BF16),
             pltpu.VMEM((512, 256), BF16),
             pltpu.VMEM((512, 128), BF16),
             pltpu.VMEM((16, 128), F32),
             pltpu.VMEM((256, 16), F32),
-            pltpu.VMEM((256, 2048), BF16),
+            pltpu.VMEM((512, 2048), BF16),
             pltpu.VMEM((32, 2048), F32),
             pltpu.VMEM((64, 8, 128), F32),
             pltpu.VMEM((8, 128), F32),
-            pltpu.VMEM((3, 8, 2, 2, 8, 128), F32),
+            pltpu.VMEM((2, 8, 2, 2, 8, 128), F32),
+            pltpu.VMEM((8, 2, 2, 16, 128), F32),
             pltpu.VMEM((2, 512, 128), F32),
             pltpu.VMEM((256, 1024), BF16),
             pltpu.VMEM((512, 1024), F32),
@@ -477,7 +497,7 @@
             pltpu.VMEM((2, 256, 256), F32),
             pltpu.VMEM((256, 256), F32),
             pltpu.VMEM((3, 256, 256), F32),
-            dma((8,)), dma((3,)), dma((3,)), dma, dma, dma((3,)), dma((4,)), dma((8,)), dma((23,)), pltpu.SemaphoreType.REGULAR,
+            dma((8,)), dma((3,)), dma((3,)), dma, dma, dma((3,)), dma((4,)), dma((8,)), dma((24,)), pltpu.SemaphoreType.REGULAR, pltpu.SemaphoreType.REGULAR,
         ],
         compiler_params=pltpu.CompilerParams(
             collective_id=0, has_side_effects=True, vmem_limit_bytes=56 * 1024 * 1024),

time: 36.6 us -> 35.8 us (0.978)
  the two profiles are of different devices: /device:TPU:65 before, /device:TPU:96 now
where the time goes in v6:
time: 35.8 us; the launch traced here: 35.7 us
  Pallas kernels  35 us (98%)
  local copies, waits for them, and re-layouts  0.71 us (2%)
    pallas_call x1, Pallas kernels, body(): pl.pallas_call(kernel, out_shape=pltpu.VMEM((1, 256, 256), F32), in_specs...  35 us

profile of v6, /device:TPU:96, one launch (start us, length us, event | category | flops | bytes accessed | tf_op | source)
XLA Modules:
  0.0 35.7 jit_solution(5399944906442377254)
XLA Ops:
  0.0 35.0 %shard_map.91 = f32[1,256,256]{2,1,0:T(8,128)S(1)} custom-call(f32[3,2,1,128,128]{4,3,2,1,0:T(8,128)} %modes_in.1, f32[1,256,256]{2,1,0:T(8,128)} %scalar.1, s32[1,2,2]{2,1,0:T(2,128)} %obstacle.1, bf16[2048,256]{1,0:T(8,128)(2,1)} %constant.12.clone.x_high_in, bf16[2048,256]{1,0:T(8,128)(2,1)} %constant.13.clone.x_low_in, ...), custom_call_target="tpu_custom_call" | custom-call | tf_op jit(solution)/shard_map/pallas_call | solution.py:465
  35.0 0.7 %copy.11 = f32[1,256,256]{2,1,0:T(8,128)} copy(f32[1,256,256]{2,1,0:T(8,128)S(1)} %shard_map.91) | data formatting | bytes 524288

commit v7 on v6

--- a/solution.py
+++ b/solution.py
@@ -14,7 +14,7 @@
 COLS = 8
 SECS = 4
 FAR_FIRST = (4, 5, 3, 2, 6, 1, 7)
-PIECES = (32,32,64,128)
+PIECES = (32,0,96,128)
 ORDER = (0,1,2)
 F32 = jnp.float32
 BF16 = jnp.bfloat16
@@ -37,7 +37,7 @@
     m = np.arange(64)
     turn = 2.0 * math.pi / 256 * ((s[:, None] * m[None, :]) % 256)
     c, d = np.cos(turn), np.sin(turn)
-    y_high, y_low = split_pair(np.block([[c, d], [d, -c]]))
+    y_high, y_low = split_pair(np.concatenate([np.block([[c[h], d[h]], [d[h], -c[h]]]) for h in (slice(0, 128), slice(128, 256))], 0))
     y_high = np.concatenate([y_high, y_high], 1)
     lanes = np.arange(128)
     turn = 2.0 * math.pi / 8 * ((np.arange(8)[:, None] * lanes[None, :]) % 8)
@@ -350,23 +350,20 @@
             high, low = split(spectra[part, pl.ds(q, 64, stride=8), :])
             rhs[pl.ds(64 * part, 64), pl.ds(128 * q, 128)] = high
             rhs[pl.ds(128 + 64 * part, 64), pl.ds(128 * q, 128)] = low
-    waves[...] = (jnp.dot(y_high[...], rhs[...], preferred_element_type=F32)
-                  + jnp.dot(y_low[...], rhs[pl.ds(0, 128), :], preferred_element_type=F32))
-
     quarter = lax.rem(lax.broadcasted_iota(jnp.int32, (16, 128), 0), 4)
     lone_real = jnp.where(quarter == 0, 1.0, jnp.where(quarter == 2, -1.0, 0.0)) * spectra[1, 0:1, :]
 
-    def combine(i, carry):
-        at = pl.multiple_of(16 * i, 16)
-        rows = pl.ds(at, 16)
+    def combine(i, number):
+        at = 16 * i
+        rows = pl.ds(128 * number + at, 16)
         real, imag = [], []
         for q in range(8):
-            re = waves[rows, pl.ds(128 * q, 128)]
+            re = waves[pl.ds(256 * number + at, 16), pl.ds(128 * q, 128)]
             if q == 0:
                 real.append(re + lone_real)
                 imag.append(None)
                 continue
-            im = waves[pl.ds(256 + at, 16), pl.ds(128 * q, 128)]
+            im = waves[pl.ds(256 * number + 128 + at, 16), pl.ds(128 * q, 128)]
             cosine, sine = twist[0, q - 1, rows, :], twist[1, q - 1, rows, :]
             real.append(re * cosine - im * sine)
             imag.append(None if q == 4 else re * sine + im * cosine)
@@ -381,22 +378,27 @@
         for r, (e, d) in enumerate(((e0, d0), (e1, d1), (e2, d2), (e3, d3))):
             fields[r, rows, :] = e + d
             fields[r + 4, rows, :] = e - d
-        return carry
-
-    lax.fori_loop(0, 16, combine, 0)
-
-    def send_fields(number, peers, steps):
+        return number
+
+    def send_fields(number, peers, steps, rows):
         def go():
             for i in steps:
                 peer = lax.rem(number + i, 8)
                 pltpu.make_async_remote_copy(
-                    fields.at[peer], velocity.at[own_part, own_half], send_sem.at[2], velocity_sem.at[own_part],
+                    fields.at[peer, rows], velocity.at[own_part, own_half, rows], send_sem.at[2], velocity_sem.at[own_part],
                     device_id=peers(i), device_id_type=MESH).start()
-            velocity[own_part, own_half] = fields[number]
+            velocity[own_part, own_half, rows] = fields[number, rows]
         return go
 
-    pl.when(plain_owner)(send_fields(row, at_row, FAR_FIRST))
-    pl.when(jnp.logical_not(plain_owner))(send_fields(col, at_col, (4, 2, 6)))
+    for number in range(2):
+        rows = pl.ds(256 * number, 256)
+        waves[rows, :] = (jnp.dot(y_high[rows, :], rhs[...], preferred_element_type=F32)
+                          + jnp.dot(y_low[rows, :], rhs[pl.ds(0, 128), :], preferred_element_type=F32))
+        for i in range(8):
+            combine(i, number)
+        rows = pl.ds(128 * number, 128)
+        pl.when(plain_owner)(send_fields(row, at_row, FAR_FIRST, rows))
+        pl.when(jnp.logical_not(plain_owner))(send_fields(col, at_col, (4, 2, 6), rows))
 
     pieces = [piece for piece in range(4) if PIECES[piece]]
     for piece in pieces:

time: 35.8 us -> 34.3 us (0.958)
  the two profiles are of different devices: /device:TPU:96 before, /device:TPU:1 now
where the time goes in v7:
time: 34.3 us; the launch traced here: 34.1 us
  Pallas kernels  33.4 us (97%)
  local copies, waits for them, and re-layouts  0.71 us (2%)
    pallas_call x1, Pallas kernels, body(): pl.pallas_call(kernel, out_shape=pltpu.VMEM((1, 256, 256), F32), in_specs...  33.4 us
    unnamed x1, local copies, waits for them, and re-layouts  0.71 us

profile of v7, /device:TPU:1, one launch (start us, length us, event | category | flops | bytes accessed | tf_op | source)
XLA Modules:
  0.0 34.1 jit_solution(4589338027610501090)
XLA Ops:
  0.0 33.4 %shard_map.91 = f32[1,256,256]{2,1,0:T(8,128)S(1)} custom-call(f32[3,2,1,128,128]{4,3,2,1,0:T(8,128)} %modes_in.1, f32[1,256,256]{2,1,0:T(8,128)} %scalar.1, s32[1,2,2]{2,1,0:T(2,128)} %obstacle.1, bf16[2048,256]{1,0:T(8,128)(2,1)} %constant.12.clone.x_high_in, bf16[2048,256]{1,0:T(8,128)(2,1)} %constant.13.clone.x_low_in, ...), custom_call_target="tpu_custom_call" | custom-call | tf_op jit(solution)/shard_map/pallas_call | solution.py:467
  33.4 0.7 %copy.11 = f32[1,256,256]{2,1,0:T(8,128)} copy(f32[1,256,256]{2,1,0:T(8,128)S(1)} %shard_map.91) | data formatting | bytes 524288

commit v8 on v7

--- a/solution.py
+++ b/solution.py
@@ -14,7 +14,7 @@
 COLS = 8
 SECS = 4
 FAR_FIRST = (4, 5, 3, 2, 6, 1, 7)
-PIECES = (32,0,96,128)
+PIECES = (32,0,112,112)
 ORDER = (0,1,2)
 F32 = jnp.float32
 BF16 = jnp.bfloat16

time: 34.3 us -> 34.3 us (level)
  no operation moved by 1% of the time
where the time goes in v8:
time: 34.3 us; the launch traced here: 34.1 us
  Pallas kernels  33.4 us (97%)
  local copies, waits for them, and re-layouts  0.71 us (2%)
    pallas_call x1, Pallas kernels, body(): pl.pallas_call(kernel, out_shape=pltpu.VMEM((1, 256, 256), F32), in_specs...  33.4 us
    unnamed x1, local copies, waits for them, and re-layouts  0.71 us

profile of v8, /device:TPU:1, one launch (start us, length us, event | category | flops | bytes accessed | tf_op | source)
XLA Modules:
  0.0 34.1 jit_solution(6231373062759178559)
XLA Ops:
  0.0 33.4 %shard_map.91 = f32[1,256,256]{2,1,0:T(8,128)S(1)} custom-call(f32[3,2,1,128,128]{4,3,2,1,0:T(8,128)} %modes_in.1, f32[1,256,256]{2,1,0:T(8,128)} %scalar.1, s32[1,2,2]{2,1,0:T(2,128)} %obstacle.1, bf16[2048,256]{1,0:T(8,128)(2,1)} %constant.12.clone.x_high_in, bf16[2048,256]{1,0:T(8,128)(2,1)} %constant.13.clone.x_low_in, ...), custom_call_target="tpu_custom_call" | custom-call | tf_op jit(solution)/shard_map/pallas_call | solution.py:467
  33.4 0.7 %copy.11 = f32[1,256,256]{2,1,0:T(8,128)} copy(f32[1,256,256]{2,1,0:T(8,128)S(1)} %shard_map.91) | data formatting | bytes 524288
